TPU v7x, 512 devices: a whole 4x8x8 slice. The times are simulated.
512 devices in a mesh: det: 128 (over y, z, core), row: 4 (over x).
Axes of the slice: x: 4, y: 8, z: 8, core: 2. Of those that a mesh axis runs over, the one named last changes fastest.
Arguments:
- science: float32 [128, 128, 768], P('det', 'row'), may hold values from -6 to 6
- template: float32 [128, 6, 128, 128], P('det', None, 'row'), may hold values from -6 to 6
- tile_source: int32 [128, 6], replicated, may hold values from 0 to 767, as said below
- offsets: int32 [2, 128, 6], P(None, 'det'), may hold values from 0 to 3
- shift_weights: float32 [2, 128, 6], P(None, 'det'), may hold values from 0 to 1
- valid_rows: int32 [128, 6], P('det'), may hold values from 32 to 128
- basis_kernels: float32 [27, 31, 31], replicated, may hold values from -0.1875 to 0.1875
- coefficients: float32 [128, 27], P('det'), may hold values from -1.25 to 1.25
- background: float32 [128], P('det'), may hold values from -4 to 4
Outputs:
- difference_tiles: float32 [128, 6, 128, 128], P('det', None, 'row')
Inputs may be any that keep to these rules, and one draw needn't show every extreme that they name: `tile_source`: entry [d, c] names slot s of sky patch p as p * 6 + s. Row d names the patches (d + j) mod 128 for j = 0 .. 3, in that order along the columns, each in one run of consecutive columns that names consecutive slots, 1 to 3 tiles long; one run of each row is exactly 3 long.
All inputs are finite; a program needn't handle non-finite values.
Results may differ from a plain program's by a relative error of at most 0.000062.
Values sent between devices are 32-bit elements; how exact they have to be, the bound alone decides.
A program may use at most 64 MiB of HBM per device.

v0:
```python
import jax
import jax.numpy as jnp
from jax import lax
from jax.sharding import PartitionSpec as P

MAXOFF = 4
SPAN = 4


def with_halo(block, sides, width):
    for axis, dim in sides:
        count = lax.axis_size(axis)
        forward = [(i, i + 1) for i in range(count - 1)]
        backward = [(target, source) for source, target in forward]
        low = lax.ppermute(
            lax.slice_in_dim(block, block.shape[dim] - width, None, axis=dim), axis, forward
        )
        high = lax.ppermute(lax.slice_in_dim(block, 0, width, axis=dim), axis, backward)
        block = jnp.concatenate([low, block, high], axis=dim)
    return block


def shifted(value, axis, steps):
    count = lax.axis_size(axis)
    pairs = [(source, (source + steps) % count) for source in range(count)]
    return lax.ppermute(value, axis, pairs)


def run_ranks(row_sources, slot_count):
    owners = row_sources // slot_count
    order = jnp.arange(row_sources.shape[0], dtype=jnp.int32)
    same_owner = owners[:, None] == owners[None, :]
    earlier = order[None, :] < order[:, None]
    ranks = jnp.sum(jnp.logical_and(same_owner, earlier).astype(jnp.int32), axis=1)
    return (owners, ranks)


def body(
    science,
    template,
    tile_source,
    offsets,
    shift_weights,
    valid_rows,
    basis_kernels,
    coefficients,
    background,
):
    highest = lax.Precision.HIGHEST
    band_rows = science.shape[1]
    columns = science.shape[2]
    tile_size = template.shape[3]
    slot_count = template.shape[1]
    tile_count = columns // tile_size
    detectors = tile_source.shape[0]
    kernel_width = basis_kernels.shape[1]
    half_width = kernel_width // 2
    capacity = tile_count // 2
    det_index = lax.axis_index("det")
    row_index = lax.axis_index("row")
    row_devices = lax.axis_size("row")
    deep_width = half_width + MAXOFF
    rank_ids = jnp.arange(capacity, dtype=jnp.int32)
    slot_range = jnp.arange(slot_count, dtype=jnp.int32)

    def send_routing(reach):
        target = (det_index - reach) % detectors
        row_sources = lax.dynamic_index_in_dim(tile_source, target, 0, keepdims=False)
        owners, ranks = run_ranks(row_sources, slot_count)
        rank_hot = jnp.logical_and(
            ranks[:, None] == rank_ids[None, :], (owners == det_index)[:, None]
        ).astype(jnp.float32)
        slot_hot = ((row_sources % slot_count)[:, None] == slot_range[None, :]).astype(jnp.float32)
        return jnp.einsum("ck,cs->ks", rank_hot, slot_hot, precision=highest)

    routings = [send_routing(reach) for reach in range(SPAN)]
    own_sources = lax.dynamic_index_in_dim(tile_source, det_index, 0, keepdims=False)
    own_owners, own_ranks = run_ranks(own_sources, slot_count)
    own_reach = (own_owners - det_index) % detectors
    reach_hot = own_reach[:, None] == jnp.arange(SPAN, dtype=jnp.int32)[None, :]
    own_rank_hot = own_ranks[:, None] == rank_ids[None, :]
    picking = jnp.logical_and(reach_hot[:, :, None], own_rank_hot[:, None, :]).astype(jnp.float32)
    stored = template[0]
    stored = with_halo(stored, (("row", 1),), deep_width)
    outgoing = [
        jnp.einsum("ks,syi->kyi", routings[reach], stored, precision=highest)
        for reach in range(SPAN)
    ]
    received = [outgoing[0]]
    for reach in range(1, SPAN):
        received.append(shifted(outgoing[reach], "det", -reach))
    incoming = jnp.stack(received)
    arranged = jnp.einsum("cjk,jkyi->yci", picking, incoming, precision=highest)
    raw_band = arranged.reshape(arranged.shape[0], columns)
    row_shift = offsets[0, 0]
    column_shift = offsets[1, 0]
    row_weight = shift_weights[0, 0]
    column_weight = shift_weights[1, 0]
    pixel_ids = jnp.arange(tile_size, dtype=jnp.int32)
    first_index = jnp.minimum(pixel_ids[None, :] + column_shift[:, None], tile_size - 1)
    second_index = jnp.minimum(pixel_ids[None, :] + column_shift[:, None] + 1, tile_size - 1)
    first_select = (pixel_ids[None, :, None] == first_index[:, None, :]).astype(jnp.float32)
    second_select = (pixel_ids[None, :, None] == second_index[:, None, :]).astype(jnp.float32)
    shift_ids = jnp.arange(MAXOFF + 1, dtype=jnp.int32)
    row_coeffs = (1.0 - row_weight)[None, :] * (shift_ids[:, None] == row_shift[None, :]).astype(
        jnp.float32
    )
    row_coeffs = row_coeffs + row_weight[None, :] * (
        shift_ids[:, None] == row_shift[None, :] + 1
    ).astype(jnp.float32)
    column_coeffs = jnp.repeat(row_coeffs, tile_size, axis=1)
    blocks = raw_band.reshape(raw_band.shape[0], tile_count, tile_size)
    left_part = jnp.einsum("ycj,cji->yci", blocks, first_select, precision=highest)
    right_part = jnp.einsum("ycj,cji->yci", blocks, second_select, precision=highest)
    mixed = (1.0 - column_weight)[None, :, None] * left_part + column_weight[
        None, :, None
    ] * right_part
    across = mixed.reshape(raw_band.shape[0], columns)
    row_total = band_rows + 2 * half_width
    result = jnp.zeros((row_total, columns), jnp.float32)
    for shift_step in range(MAXOFF + 1):
        result = (
            result
            + column_coeffs[shift_step][None, :]
            * across[MAXOFF + shift_step : MAXOFF + shift_step + row_total]
        )
    warped_ext = result
    global_rows = (
        row_index * band_rows - half_width + jnp.arange(band_rows + 2 * half_width, dtype=jnp.int32)
    )
    inside = jnp.logical_and(global_rows >= 0, global_rows < row_devices * band_rows)
    warped_ext = jnp.where(inside[:, None], warped_ext, jnp.float32(0.0))
    kernel = jnp.einsum("k,kab->ab", coefficients[0], basis_kernels, precision=highest)
    tap_ids = jnp.arange(kernel_width, dtype=jnp.int32)
    lead_hot = (
        pixel_ids[:, None, None] - pixel_ids[None, :, None] == tap_ids[None, None, :]
    ).astype(jnp.float32)
    lead_bands = jnp.einsum("jib,ab->aji", lead_hot, kernel, precision=highest)
    trail_ids = jnp.arange(kernel_width - 1, dtype=jnp.int32)
    trail_hot = (
        tile_size + trail_ids[:, None, None] - pixel_ids[None, :, None] == tap_ids[None, None, :]
    ).astype(jnp.float32)
    trail_bands = jnp.einsum("jib,ab->aji", trail_hot, kernel, precision=highest)
    padded = jnp.pad(warped_ext, ((0, 0), (half_width, tile_size - half_width)))

    def kernel_row(tap_row, summed):
        rows_here = lax.dynamic_slice_in_dim(padded, tap_row, band_rows, 0)
        main_part = rows_here[:, :columns].reshape(band_rows, tile_count, tile_size)
        next_part = rows_here[:, tile_size:].reshape(band_rows, tile_count, tile_size)[
            :, :, : kernel_width - 1
        ]
        lead_now = lax.dynamic_index_in_dim(lead_bands, tap_row, 0, keepdims=False)
        trail_now = lax.dynamic_index_in_dim(trail_bands, tap_row, 0, keepdims=False)
        summed = summed + jnp.einsum("ycj,ji->yci", main_part, lead_now, precision=highest)
        return summed + jnp.einsum("ycj,ji->yci", next_part, trail_now, precision=highest)

    modelled = lax.fori_loop(
        0, kernel_width, kernel_row, jnp.zeros((band_rows, tile_count, tile_size), jnp.float32)
    )
    residual_image = science[0].reshape(band_rows, tile_count, tile_size) - modelled - background[0]
    band_global = row_index * band_rows + jnp.arange(band_rows, dtype=jnp.int32)
    usable = band_global[:, None] < valid_rows[0][None, :]
    residual_image = jnp.where(usable[:, :, None], residual_image, jnp.float32(0.0))
    returning = jnp.einsum("cjk,yci->jkyi", picking, residual_image, precision=highest)
    returned = [returning[0]]
    for reach in range(1, SPAN):
        returned.append(shifted(returning[reach], "det", reach))
    summed = jnp.zeros(stored.shape[:1] + (band_rows, tile_size), jnp.float32)
    tallies = jnp.zeros((slot_count,), jnp.float32)
    for reach in range(SPAN):
        summed = summed + jnp.einsum(
            "ks,kyi->syi", routings[reach], returned[reach], precision=highest
        )
        tallies = tallies + jnp.sum(routings[reach], axis=0)
    result = summed / jnp.maximum(tallies, 1.0)[:, None, None]
    return result[None]


def solution(mesh):
    in_specs = (
        P("det", "row", None),
        P("det", None, "row", None),
        P(),
        P(None, "det", None),
        P(None, "det", None),
        P("det", None),
        P(),
        P("det", None),
        P("det"),
    )
    out_specs = P("det", None, "row", None)
    return jax.shard_map(body, mesh=mesh, in_specs=in_specs, out_specs=out_specs, check_vma=False)
```

profile of v0, /device:TPU:1, one launch (start us, length us, event | category | flops | bytes accessed | tf_op | source)
XLA Modules:
  0.0 111.6 jit_solution(3103127253902588699)
XLA Ops:
  0.0 1.0 copy.115
  1.0 3.9 %collective-permute-start = (f32[6,19,128]{2,0,1:T(8,128)S(1)}, f32[6,19,128]{2,0,1:T(8,128)S(1)}, u32[]{:S(2)}, u32[]{:S(2)}) collective-permute-start(f32[6,19,128]{2,0,1:T(8,128)S(1)} %get-tuple-element.178), channel_id=1, source_target_pairs={{0,1},{1,2},{2,3},{4,5},{5,6},{6,7},{8,9},{9,10},{10,11},{12,13},{... | collective-permute-start | bytes 175112 | tf_op jit(solution)/shard_map/ppermute | solution.py:15
  5.0 1.3 %collective-permute-start.1 = (f32[6,19,128]{2,0,1:T(8,128)S(1)}, f32[6,19,128]{2,0,1:T(8,128)S(1)}, u32[]{:S(2)}, u32[]{:S(2)}) collective-permute-start(f32[6,19,128]{2,0,1:T(8,128)S(1)} %get-tuple-element.179), channel_id=1, source_target_pairs={{1,0},{2,1},{3,2},{5,4},{6,5},{7,6},{9,8},{10,9},{11,10},{13,12},{... | collective-permute-start | bytes 175112 | tf_op jit(solution)/shard_map/ppermute | solution.py:18
  6.4 0.7 broadcast_subtract_fusion.1
  7.0 0.7 slice_bitcast_fusion.7
  7.7 0.7 slice_bitcast_fusion.8
  8.4 0.7 broadcast_add_fusion
  9.1 1.1 %fusion.111 = (pred[6]{0:T(512)(128)(4,1)S(1)}, pred[1,6]{0,1:T(8,128)(4,1)S(1)}, pred[6]{0:T(512)(128)(4,1)S(1)}, pred[1,6]{0,1:T(8,128)(4,1)S(1)}, pred[6]{0:T...) fusion(s32[128,6]{0,1:T(8,128)} %param.13, ...), kind=kLoop, calls=%fused_computation.208 | loop fusion | flops 78 | bytes 200 | tf_op jit(solution)/shard_map/jit(floor_divide)/ne | solution.py:30
  10.2 1.3 %fusion.97 = (s32[6]{0:T(128)S(1)}, s32[6]{0:T(128)S(1)}, s32[6]{0:T(128)S(1)}, s32[6]{0:T(128)S(1)}, s32[6]{0:T(128)S(1)}, /*index=5*/s32[6]{0:T(128)S(1)}, s32...) fusion(s32[128,6]{0,1:T(8,128)} %param.13, ...), kind=kLoop, calls=%fused_computation.175 | loop fusion | flops 162 | bytes 506 | tf_op jit(solution)/shard_map/jit(floor_divide)/div | solution.py:30
  12.3 1.2 %fusion.17 = f32[1,31,31]{2,0,1:T(1,128)S(1)} fusion(f32[27,31,31]{2,1,0:T(8,128)S(1)} %copy-done, f32[1,27]{1,0:T(1,128)} %param.18), kind=kOutput, calls=%fused_computation.30 | convolution fusion | flops 311364 | bytes 107740 | tf_op jit(solution)/shard_map/k,kab->ab/dot_general | solution.py:133
  13.6 1.4 %fusion.3 = f32[31,128,128]{2,0,1:T(8,128)S(1)} fusion(pred[128,128,31]{1,0,2:T(32,128)(4,1)S(1)} %iota_compare_fusion, f32[1,31,31]{2,0,1:T(1,128)S(1)} %fusion.17), kind=kOutput, calls=%fused_computation.9 | convolution fusion | flops 188940288 | bytes 2543364 | tf_op jit(solution)/shard_map/jib,ab->aji/dot_general | solution.py:138
  14.9 1.1 fusion.19
  18.9 0.4 fusion.41
  19.2 6.1 %collective-permute-start.2 = (f32[3,70,128]{2,0,1:T(4,128)S(1)}, f32[3,70,128]{2,0,1:T(4,128)S(1)}, u32[]{:S(2)}, u32[]{:S(2)}) collective-permute-start(f32[3,70,128]{2,0,1:T(4,128)S(1)} %fusion.41), channel_id=1, source_target_pairs={{0,508},{4,0},{8,4},{12,8},{16,12},{20,16},{24,20},{28,24},{32,28}... | collective-permute-start | bytes 322568 | tf_op jit(solution)/shard_map/ppermute | solution.py:26
  25.4 0.4 fusion.40
  25.7 10.3 %collective-permute-start.3 = (f32[3,70,128]{2,0,1:T(4,128)S(1)}, f32[3,70,128]{2,0,1:T(4,128)S(1)}, u32[]{:S(2)}, u32[]{:S(2)}) collective-permute-start(f32[3,70,128]{2,0,1:T(4,128)S(1)} %fusion.40), channel_id=1, source_target_pairs={{0,504},{4,508},{8,0},{12,4},{16,8},{20,12},{24,16},{28,20},{32,24... | collective-permute-start | bytes 322568 | tf_op jit(solution)/shard_map/ppermute | solution.py:26
  36.1 0.4 fusion.39
  36.4 2.4 %collective-permute-start.4 = (f32[3,70,128]{2,0,1:T(4,128)S(1)}, f32[3,70,128]{2,0,1:T(4,128)S(1)}, u32[]{:S(2)}, u32[]{:S(2)}) collective-permute-start(f32[3,70,128]{2,0,1:T(4,128)S(1)} %fusion.39), channel_id=1, source_target_pairs={{0,500},{4,504},{8,508},{12,0},{16,4},{20,8},{24,12},{28,16},{32,2... | collective-permute-start | bytes 322568 | tf_op jit(solution)/shard_map/ppermute | solution.py:26
  38.8 0.4 convolution_bitcast_fusion.1
  39.2 5.4 %collective-permute-done.4 = f32[3,70,128]{2,0,1:T(4,128)S(1)} collective-permute-done((f32[3,70,128]{2,0,1:T(4,128)S(1)}, f32[3,70,128]{2,0,1:T(4,128)S(1)}, u32[]{:S(2)}, u32[]{:S(2)}) %collective-permute-start.4) | collective-permute-done | bytes 107552 | tf_op jit(solution)/shard_map/ppermute | solution.py:26
  44.6 0.5 convolution_bitcast_fusion
  45.2 0.4 convolution_multiply_fusion.1
  45.5 0.4 fusion.6
  47.2 50.4 %while.14 = (s32[]{:T(128)}, f32[32,6,128]{2,0,1:T(8,128)S(1)}, f32[62,896]{1,0:T(8,128)S(1)}, f32[31,128,128]{2,0,1:T(8,128)S(1)}, f32[31,30,128]{2,0,1:T(8,128)}, /*index=5*/s32[]{:T(128)}, s32[]{:T(128)}, s32[]{}) while((s32[]{:T(128)}, f32[32,6,128]{2,0,1:T(8,128)S(1)}, f32[62,896]{1,0:T(8,128)S(1)}, ...), condition=%wide.region_6.7_spmd.clone, body=%wide.region_5.6_spmd.clone.sunk | while | flops 46669828 | bytes 1347195 | solution.py:157
  47.7 0.9 constant_dynamic-slice_fusion.5
  49.3 0.9 constant_dynamic-slice_fusion.5
  51.0 0.9 constant_dynamic-slice_fusion.5
  52.6 0.9 constant_dynamic-slice_fusion.5
  54.2 0.9 constant_dynamic-slice_fusion.5
  55.8 0.9 constant_dynamic-slice_fusion.5
  57.5 0.9 constant_dynamic-slice_fusion.5
  59.1 0.9 constant_dynamic-slice_fusion.5
  60.7 0.9 constant_dynamic-slice_fusion.5
  62.3 0.9 constant_dynamic-slice_fusion.5
  64.0 0.9 constant_dynamic-slice_fusion.5
  65.6 0.9 constant_dynamic-slice_fusion.5
  67.2 0.9 constant_dynamic-slice_fusion.5
  68.8 0.9 constant_dynamic-slice_fusion.5
  70.5 0.9 constant_dynamic-slice_fusion.5
  72.1 0.9 constant_dynamic-slice_fusion.5
  73.7 0.9 constant_dynamic-slice_fusion.5
  75.3 0.9 constant_dynamic-slice_fusion.5
  77.0 0.9 constant_dynamic-slice_fusion.5
  78.6 0.9 constant_dynamic-slice_fusion.5
  80.2 0.9 constant_dynamic-slice_fusion.5
  81.8 0.9 constant_dynamic-slice_fusion.5
  83.5 0.9 constant_dynamic-slice_fusion.5
  85.1 0.9 constant_dynamic-slice_fusion.5
  86.7 0.9 constant_dynamic-slice_fusion.5
  88.3 0.9 constant_dynamic-slice_fusion.5
  90.0 0.9 constant_dynamic-slice_fusion.5
  91.6 0.9 constant_dynamic-slice_fusion.5
  93.2 0.9 constant_dynamic-slice_fusion.5
  94.8 0.9 constant_dynamic-slice_fusion.5
  96.5 0.9 constant_dynamic-slice_fusion.5
  97.6 0.3 fusion.25
  98.1 2.1 %collective-permute-start.5 = (f32[3,32,128]{2,1,0:T(8,128)S(1)}, f32[3,32,128]{2,1,0:T(8,128)S(1)}, u32[]{:S(2)}, u32[]{:S(2)}) collective-permute-start(f32[3,32,128]{2,1,0:T(8,128)S(1)} %bitcast.158), channel_id=1, source_target_pairs={{0,4},{4,8},{8,12},{12,16},{16,20},{20,24},{24,28},{28,32},{32,36}... | collective-permute-start | bytes 147464 | tf_op jit(solution)/shard_map/ppermute | solution.py:26
  100.5 1.9 %collective-permute-start.7 = (f32[3,32,128]{2,1,0:T(8,128)S(1)}, f32[3,32,128]{2,1,0:T(8,128)S(1)}, u32[]{:S(2)}, u32[]{:S(2)}) collective-permute-start(f32[3,32,128]{2,1,0:T(8,128)S(1)} %bitcast.157), channel_id=1, source_target_pairs={{0,12},{4,16},{8,20},{12,24},{16,28},{20,32},{24,36},{28,40},{32,4... | collective-permute-start | bytes 147464 | tf_op jit(solution)/shard_map/ppermute | solution.py:26
  102.4 1.9 %collective-permute-start.6 = (f32[3,32,128]{2,1,0:T(8,128)S(1)}, f32[3,32,128]{2,1,0:T(8,128)S(1)}, u32[]{:S(2)}, u32[]{:S(2)}) collective-permute-start(f32[3,32,128]{2,1,0:T(8,128)S(1)} %bitcast.156), channel_id=1, source_target_pairs={{0,8},{4,12},{8,16},{12,20},{16,24},{20,28},{24,32},{28,36},{32,40... | collective-permute-start | bytes 147464 | tf_op jit(solution)/shard_map/ppermute | solution.py:26
  104.4 0.3 convolution_add_fusion.3
  104.7 4.5 %collective-permute-done.7 = f32[3,32,128]{2,1,0:T(8,128)S(1)} collective-permute-done((f32[3,32,128]{2,1,0:T(8,128)S(1)}, f32[3,32,128]{2,1,0:T(8,128)S(1)}, u32[]{:S(2)}, u32[]{:S(2)}) %collective-permute-start.7) | collective-permute-done | bytes 49184 | tf_op jit(solution)/shard_map/ppermute | solution.py:26
  109.6 1.0 collective-permute-done.6
  110.6 0.3 fusion.9
  110.9 0.7 copy.56
  (221 shorter events, 24.9 us)
Async XLA Ops:
  0.0 12.3 %copy-start = (f32[27,31,31]{2,1,0:T(8,128)S(1)}, f32[27,31,31]{2,1,0:T(8,128)}, u32[]{:S(2)}) copy-start(f32[27,31,31]{2,1,0:T(8,128)} %param.17) | copy-start | bytes 311368
  1.0 17.8 %collective-permute-start = (f32[6,19,128]{2,0,1:T(8,128)S(1)}, f32[6,19,128]{2,0,1:T(8,128)S(1)}, u32[]{:S(2)}, u32[]{:S(2)}) collective-permute-start(f32[6,19,128]{2,0,1:T(8,128)S(1)} %get-tuple-element.178), channel_id=1, source_target_pairs={{0,1},{1,2},{2,3},{4,5},{5,6},{6,7},{8,9},{9,10},{10,11},{12,13},{... | collective-permute-start | bytes 175112 | tf_op jit(solution)/shard_map/ppermute | solution.py:15
  5.0 13.9 %collective-permute-start.1 = (f32[6,19,128]{2,0,1:T(8,128)S(1)}, f32[6,19,128]{2,0,1:T(8,128)S(1)}, u32[]{:S(2)}, u32[]{:S(2)}) collective-permute-start(f32[6,19,128]{2,0,1:T(8,128)S(1)} %get-tuple-element.179), channel_id=1, source_target_pairs={{1,0},{2,1},{3,2},{5,4},{6,5},{7,6},{9,8},{10,9},{11,10},{13,12},{... | collective-permute-start | bytes 175112 | tf_op jit(solution)/shard_map/ppermute | solution.py:18
  11.9 4.1 %copy-start.1 = (f32[1,32,768]{2,1,0:T(8,128)S(1)}, f32[1,32,768]{2,1,0:T(8,128)}, u32[]{:S(2)}) copy-start(f32[1,32,768]{2,1,0:T(8,128)} %param.11) | copy-start | bytes 294916
  12.2 5.4 %copy-start.2 = (s32[1,6]{1,0:T(1,128)S(1)}, s32[1,6]{1,0:T(1,128)}, u32[]{:S(2)}) copy-start(s32[1,6]{1,0:T(1,128)} %param.16) | copy-start | bytes 76
  19.2 20.0 %collective-permute-start.2 = (f32[3,70,128]{2,0,1:T(4,128)S(1)}, f32[3,70,128]{2,0,1:T(4,128)S(1)}, u32[]{:S(2)}, u32[]{:S(2)}) collective-permute-start(f32[3,70,128]{2,0,1:T(4,128)S(1)} %fusion.41), channel_id=1, source_target_pairs={{0,508},{4,0},{8,4},{12,8},{16,12},{20,16},{24,20},{28,24},{32,28}... | collective-permute-start | bytes 322568 | tf_op jit(solution)/shard_map/ppermute | solution.py:26
  25.7 13.5 %collective-permute-start.3 = (f32[3,70,128]{2,0,1:T(4,128)S(1)}, f32[3,70,128]{2,0,1:T(4,128)S(1)}, u32[]{:S(2)}, u32[]{:S(2)}) collective-permute-start(f32[3,70,128]{2,0,1:T(4,128)S(1)} %fusion.40), channel_id=1, source_target_pairs={{0,504},{4,508},{8,0},{12,4},{16,8},{20,12},{24,16},{28,20},{32,24... | collective-permute-start | bytes 322568 | tf_op jit(solution)/shard_map/ppermute | solution.py:26
  36.4 8.2 %collective-permute-start.4 = (f32[3,70,128]{2,0,1:T(4,128)S(1)}, f32[3,70,128]{2,0,1:T(4,128)S(1)}, u32[]{:S(2)}, u32[]{:S(2)}) collective-permute-start(f32[3,70,128]{2,0,1:T(4,128)S(1)} %fusion.39), channel_id=1, source_target_pairs={{0,500},{4,504},{8,508},{12,0},{16,4},{20,8},{24,12},{28,16},{32,2... | collective-permute-start | bytes 322568 | tf_op jit(solution)/shard_map/ppermute | solution.py:26
  98.1 6.3 %collective-permute-start.5 = (f32[3,32,128]{2,1,0:T(8,128)S(1)}, f32[3,32,128]{2,1,0:T(8,128)S(1)}, u32[]{:S(2)}, u32[]{:S(2)}) collective-permute-start(f32[3,32,128]{2,1,0:T(8,128)S(1)} %bitcast.158), channel_id=1, source_target_pairs={{0,4},{4,8},{8,12},{12,16},{16,20},{20,24},{24,28},{28,32},{32,36}... | collective-permute-start | bytes 147464 | tf_op jit(solution)/shard_map/ppermute | solution.py:26
  100.5 8.7 %collective-permute-start.7 = (f32[3,32,128]{2,1,0:T(8,128)S(1)}, f32[3,32,128]{2,1,0:T(8,128)S(1)}, u32[]{:S(2)}, u32[]{:S(2)}) collective-permute-start(f32[3,32,128]{2,1,0:T(8,128)S(1)} %bitcast.157), channel_id=1, source_target_pairs={{0,12},{4,16},{8,20},{12,24},{16,28},{20,32},{24,36},{28,40},{32,4... | collective-permute-start | bytes 147464 | tf_op jit(solution)/shard_map/ppermute | solution.py:26
  102.4 8.2 %collective-permute-start.6 = (f32[3,32,128]{2,1,0:T(8,128)S(1)}, f32[3,32,128]{2,1,0:T(8,128)S(1)}, u32[]{:S(2)}, u32[]{:S(2)}) collective-permute-start(f32[3,32,128]{2,1,0:T(8,128)S(1)} %bitcast.156), channel_id=1, source_target_pairs={{0,8},{4,12},{8,16},{12,20},{16,24},{20,28},{24,32},{28,36},{32,40... | collective-permute-start | bytes 147464 | tf_op jit(solution)/shard_map/ppermute | solution.py:26
where the time goes:
time: 114 us; the launch traced here: 112 us
  local copies, waits for them, and re-layouts  39.3 us (34%)
  starting transfers between devices  29.9 us (26%)
  matrix products  23 us (20%)
  waiting for transfers between devices  11 us (10%)
  other arithmetic  5.43 us (5%)
  loops' own time  1.73 us (2%)
  between operations  1.22 us (1%)
    dynamic_slice x31, local copies, waits for them, and re-layouts, kernel_row(): lax.dynamic_index_in_dim(trail_bands, tap_row, 0, keepdims=False)  28.6 us
    ppermute x6, starting transfers between devices, shifted(): return lax.ppermute(value, axis, pairs)  24.7 us
    ppermute x6, waiting for transfers between devices, shifted(): return lax.ppermute(value, axis, pairs)  11 us
    dot_general x31, matrix products, kernel_row(): jnp.einsum('ycj,ji->yci', main_part, lead_now, precision=highest)  7.22 us
    dot_general x31, matrix products, kernel_row(): jnp.einsum('ycj,ji->yci', next_part, trail_now, precision=highest)  6.69 us
    ppermute x1, starting transfers between devices, with_halo(): lax.ppermute(lax.slice_in_dim(block, block.shape[dim] - width, None, axis...  3.94 us
    slice x31, local copies, waits for them, and re-layouts, kernel_row(): rows_here[:, tile_size:].reshape(band_rows, tile_count, tile_size)  3.2 us
    dynamic_slice x31, local copies, waits for them, and re-layouts, kernel_row(): lead_now = lax.dynamic_index_in_dim(lead_bands, tap_row, 0, keepdims=False)  2.45 us
  transfers between devices with their start and end apart: 8, of which 3 were waited for; matrix products, arithmetic and copies ran while one was open for 12% of the time, Pallas kernels for 0%

commit v1 on v0

v1 whole, which is shorter than its diff:
```python
import functools

import jax
import jax.numpy as jnp
from jax import lax
from jax.experimental import pallas as pl
from jax.experimental.pallas import tpu as pltpu
from jax.sharding import PartitionSpec as P

MESH = pl.DeviceIdType.MESH
SPAN = 4
CAP = 3
TILES = 6
TILE = 128
BAND = 32
ABOVE = 16
BELOW = 24
DEEP = ABOVE + BAND + BELOW
KW = 31
HALF = 15
NB = 27
MAXOFF = 4
ZERO_TILE = 12


def split(x):
    high = x.astype(jnp.bfloat16).astype(jnp.float32)
    return high, x - high


def kernel(
    det_count,
    row_count,
    science,
    template,
    sources,
    offsets,
    weights,
    valid,
    basis,
    coefs,
    background,
    out,
    own,
    tiles,
    edges,
    images,
    seen,
    bands,
    taps,
    taps_back,
    floats,
    ints,
    float_s,
    int_s,
    local_sem,
    send_sem,
    recv_sem,
):
    p = lax.axis_index("det")
    r = lax.axis_index("row")

    def det(j):
        return lax.rem(p + (j + det_count), det_count)

    def row(j):
        return lax.rem(r + (j + row_count), row_count)

    peers = [(det(j), r) for j in (1, -1, 2, -2, 3, -3)]
    peers += [(p, row(1)), (p, row(-1))]
    peers += [(det(j), row(i)) for j in (1, -1) for i in (1, -1)]
    barrier = pltpu.get_barrier_semaphore()
    for peer in peers:
        pl.semaphore_signal(barrier, inc=1, device_id=peer, device_id_type=MESH)

    load_own = pltpu.make_async_copy(template.at[0], own, local_sem.at[0])
    load_tiles = pltpu.make_async_copy(
        template.at[0], tiles.at[pl.ds(0, TILES), pl.ds(ABOVE, BAND), :], local_sem.at[1]
    )
    load_seen = pltpu.make_async_copy(
        science.at[0, :, pl.ds(0, CAP * TILE)], seen.at[0], local_sem.at[2]
    )
    load_own.start()
    load_tiles.start()
    load_seen.start()

    runs = []
    for q in range(SPAN):
        d = det(-q)
        start = jnp.int32(0)
        length = jnp.int32(0)
        for c in range(TILES):
            reach = lax.rem(sources[c, d] // TILES - d + det_count, det_count)
            start = start + jnp.where(reach < q, 1, 0)
            length = length + jnp.where(reach == q, 1, 0)
        start = jnp.clip(start, 0, TILES - 1)
        first = jnp.clip(sources[start, d] - p * TILES, 0, TILES - 1)
        runs.append((start, length, first))

    lane = lax.broadcasted_iota(jnp.int32, (1, TILE), 1)
    packed = jnp.zeros((1, TILE), jnp.float32)
    whole = jnp.zeros((1, TILE), jnp.int32)
    for k in range(NB):
        packed = jnp.where(lane == k, coefs[0, k], packed)
    packed = jnp.where(lane == NB, background[0], packed)
    for c in range(TILES):
        packed = jnp.where(lane == 28 + c, weights[0, 0, c], packed)
        packed = jnp.where(lane == 34 + c, weights[1, 0, c], packed)
        whole = jnp.where(lane == c, offsets[0, 0, c], whole)
        whole = jnp.where(lane == 6 + c, offsets[1, 0, c], whole)
        whole = jnp.where(lane == 12 + c, valid[0, c], whole)
    floats[0] = packed
    ints[0] = whole

    tiles[ZERO_TILE] = jnp.zeros((DEEP, TILE), jnp.float32)
    load_own.wait()
    for j in range(CAP):
        start, length, first = runs[j]
        edges[0, j] = own[jnp.clip(first + length - 1, 0, TILES - 1)]
        start, length, first = runs[j + 1]
        edges[1, j] = own[first]

    sub = lax.broadcasted_iota(jnp.int32, (8, TILE), 0)
    across = lax.broadcasted_iota(jnp.int32, (8, TILE), 1)
    rows128 = lax.broadcasted_iota(jnp.int32, (TILE, TILE), 0)
    cols128 = lax.broadcasted_iota(jnp.int32, (TILE, TILE), 1)
    mirror = jnp.where(lax.rem(rows128 + cols128, TILE) == 0, 1.0, 0.0).astype(jnp.float32)
    taps[...] = jnp.zeros((BAND, TILE), jnp.float32)

    def build(q, coefficient):
        total = coefficient(0) * basis[0]
        for k in range(1, NB):
            total = total + coefficient(k) * basis[k]
        taps[pl.ds(0, KW), pl.ds(0, KW)] = total
        high, low = split(taps[...])
        both = jnp.dot(
            jnp.concatenate([high, low], axis=0), mirror, preferred_element_type=jnp.float32
        )
        taps_back[...] = both[:BAND] + both[BAND:]
        for a in range(KW):
            line = jnp.broadcast_to(taps_back[pl.ds(a, 1), :], (8, TILE))
            block = pltpu.roll(line, 0, 1, stride=1, stride_axis=0)
            for jb in range(TILE // 8):
                turned = block if jb == 0 else pltpu.roll(block, 8 * jb, 1)
                high, low = split(turned)
                if jb < 4:
                    lead = across <= sub + 8 * jb
                    lead_high, lead_low = jnp.where(lead, high, 0.0), jnp.where(lead, low, 0.0)
                    bands[q, a, pl.ds(TILE + 8 * jb, 8), pl.ds(0, TILE)] = high - lead_high
                    bands[q, a, pl.ds(TILE + 8 * jb, 8), pl.ds(TILE, TILE)] = low - lead_low
                    high, low = lead_high, lead_low
                bands[q, a, pl.ds(8 * jb, 8), pl.ds(0, TILE)] = high
                bands[q, a, pl.ds(8 * jb, 8), pl.ds(TILE, TILE)] = low

    build(0, lambda k: coefs[0, k])

    load_tiles.wait()
    pl.semaphore_wait(barrier, len(peers))

    copies = []

    def send(src, dst, peer):
        i = len(copies)
        copy = pltpu.make_async_remote_copy(
            src_ref=src,
            dst_ref=dst,
            send_sem=send_sem.at[i],
            recv_sem=recv_sem.at[i],
            device_id=peer,
            device_id_type=MESH,
        )
        copy.start()
        copies.append(copy)

    for j in range(1, SPAN):
        send(floats.at[0], floats.at[j], (det(j), r))
        send(ints.at[0], ints.at[j], (det(j), r))
    low_rows, high_rows = pl.ds(0, ABOVE), pl.ds(ABOVE + BAND, BELOW)
    for side, j, at in ((0, 1, 6), (1, -1, 9)):
        send(edges.at[side], tiles.at[pl.ds(at, CAP), pl.ds(ABOVE, BAND), :], (det(j), r))
        send(
            edges.at[side, :, pl.ds(0, BELOW), :],
            tiles.at[pl.ds(at, CAP), high_rows, :],
            (det(j), row(-1)),
        )
        send(
            edges.at[side, :, pl.ds(BAND - ABOVE, ABOVE), :],
            tiles.at[pl.ds(at, CAP), low_rows, :],
            (det(j), row(1)),
        )
    send(own.at[:, pl.ds(0, BELOW), :], tiles.at[pl.ds(0, TILES), high_rows, :], (p, row(-1)))
    send(
        own.at[:, pl.ds(BAND - ABOVE, ABOVE), :],
        tiles.at[pl.ds(0, TILES), low_rows, :],
        (p, row(1)),
    )
    for j in range(1, SPAN):
        send(
            science.at[0, :, pl.ds(j * TILE, CAP * TILE)],
            seen.at[j],
            (det(j), r),
        )

    for copy in copies[:6]:
        copy.wait_recv()
    to_float = pltpu.make_async_copy(floats, float_s, local_sem.at[3])
    to_int = pltpu.make_async_copy(ints, int_s, local_sem.at[4])
    to_float.start()
    to_int.start()
    to_float.wait()
    to_int.wait()
    for q in range(1, SPAN):
        build(q, lambda k, q=q: float_s[q, 0, k])
    for copy in copies[6:14]:
        copy.wait_recv()

    eight = lax.broadcasted_iota(jnp.int32, (2 * BAND, TILE), 0)
    wide = lax.broadcasted_iota(jnp.int32, (2 * BAND, TILE), 1)
    line_at = eight + (r * BAND - HALF)
    tail = wide < HALF
    for q in range(SPAN):
        start, length, first = runs[q]
        before = None
        for m in range(CAP + 2):
            c = jnp.clip(start + (m - 1), 0, TILES - 1)
            row_shift = jnp.clip(int_s[q, 0, c], 0, MAXOFF - 1)
            col_shift = int_s[q, 0, 6 + c]
            row_weight, col_weight = float_s[q, 0, 28 + c], float_s[q, 0, 34 + c]
            if m == 0:
                index = 5 + q if q > 0 else ZERO_TILE
            else:
                right = 9 + q if q < SPAN - 1 else ZERO_TILE
                index = jnp.where(
                    m <= length, first + (m - 1), jnp.where(m == length + 1, right, ZERO_TILE)
                )
                index = jnp.clip(index, 0, ZERO_TILE)
            upper = tiles[index, pl.ds(1 + row_shift, 2 * BAND), :]
            lower = tiles[index, pl.ds(2 + row_shift, 2 * BAND), :]
            limit = row_count * BAND - row_shift
            upper = jnp.where(line_at < limit, (1.0 - row_weight) * upper, 0.0)
            lower = jnp.where(line_at < limit - 1, row_weight * lower, 0.0)
            mixed = jnp.where(line_at >= 0, upper + lower, 0.0)
            last = jnp.broadcast_to(mixed[:, TILE - 1 :], (2 * BAND, TILE))
            left = pltpu.roll(mixed, HALF - col_shift, 1)
            left = jnp.where(tail & (wide > HALF - 1 - col_shift), last, left)
            following = pltpu.roll(mixed, HALF - 1 - col_shift, 1)
            following = jnp.where(tail & (wide > HALF - 2 - col_shift), last, following)
            now = (1.0 - col_weight) * left + col_weight * following
            if m > 0:
                high, low = split(jnp.where(tail, before, now))
                images[q, 0, m - 1] = high
                images[q, 1, m - 1] = low
            before = now

    rest = jnp.zeros((2 * TILE - TILE - BAND, 2 * TILE), jnp.float32)
    sums = []
    for pair in range(SPAN // 2):
        accs = [None, None]
        for a in range(KW):
            for i in range(2):
                q = 2 * pair + i
                blocks = []
                for part in range(2):
                    views = [images[q, part, k, pl.ds(a, BAND), :] for k in range(CAP + 1)]
                    blocks += [
                        jnp.concatenate([views[k], views[k + 1]], axis=1) for k in range(CAP)
                    ]
                band = jnp.concatenate([bands[q, a], rest], axis=0)
                term = jnp.dot(
                    jnp.concatenate(blocks, axis=0), band, preferred_element_type=jnp.float32
                )
                accs[i] = term if accs[i] is None else accs[i] + term
        sums += accs

    load_seen.wait()
    for copy in copies[14:]:
        copy.wait_recv()

    down = lax.broadcasted_iota(jnp.int32, (BAND, TILE), 0) + r * BAND
    parts = []
    for q in range(SPAN):
        start, length, first = runs[q]
        for k in range(CAP):
            acc = sums[q]
            at = k * BAND
            model = acc[at : at + BAND, :TILE] + acc[at : at + BAND, TILE:]
            at += CAP * BAND
            model = model + (acc[at : at + BAND, :TILE] + acc[at : at + BAND, TILE:])
            pixels = seen[q, :, pl.ds(k * TILE, TILE)]
            if k == 0 and q > 0:
                pixels = jnp.where(start == q, pixels, seen[q, :, pl.ds(2 * TILE, TILE)])
            c = jnp.clip(start + k, 0, TILES - 1)
            residual = jnp.where(
                down < int_s[q, 0, 12 + c], pixels - model - float_s[q, 0, NB], 0.0
            )
            parts.append((jnp.where(k < length, first + k, -1), residual))
    for s in range(TILES):
        total = jnp.zeros((BAND, TILE), jnp.float32)
        tally = jnp.float32(0.0)
        for slot, residual in parts:
            total = total + jnp.where(slot == s, residual, 0.0)
            tally = tally + jnp.where(slot == s, 1.0, 0.0)
        out[0, s] = total / jnp.maximum(tally, 1.0)

    for copy in copies:
        copy.wait_send()


def solution(mesh):
    det_count, row_count = mesh.shape["det"], mesh.shape["row"]

    def body(
        science, template, sources, offsets, weights, valid, basis, coefs, background
    ):
        smem = pl.BlockSpec(memory_space=pltpu.SMEM)
        vmem = pl.BlockSpec(memory_space=pltpu.VMEM)
        hbm = pl.BlockSpec(memory_space=pl.ANY)
        return pl.pallas_call(
            functools.partial(kernel, det_count, row_count),
            out_shape=jax.ShapeDtypeStruct(template.shape, jnp.float32),
            in_specs=[hbm, hbm, smem, smem, smem, smem, vmem, smem, smem],
            out_specs=vmem,
            scratch_shapes=[
                pltpu.VMEM((TILES, BAND, TILE), jnp.float32),
                pltpu.VMEM((ZERO_TILE + 1, DEEP, TILE), jnp.float32),
                pltpu.VMEM((2, CAP, BAND, TILE), jnp.float32),
                pltpu.VMEM((SPAN, 2, CAP + 1, 2 * BAND, TILE), jnp.float32),
                pltpu.VMEM((SPAN, BAND, CAP * TILE), jnp.float32),
                pltpu.VMEM((SPAN, KW, TILE + BAND, 2 * TILE), jnp.float32),
                pltpu.VMEM((BAND, TILE), jnp.float32),
                pltpu.VMEM((BAND, TILE), jnp.float32),
                pltpu.VMEM((SPAN, 1, TILE), jnp.float32),
                pltpu.VMEM((SPAN, 1, TILE), jnp.int32),
                pltpu.SMEM((SPAN, 1, TILE), jnp.float32),
                pltpu.SMEM((SPAN, 1, TILE), jnp.int32),
                pltpu.SemaphoreType.DMA((5,)),
                pltpu.SemaphoreType.DMA((17,)),
                pltpu.SemaphoreType.DMA((17,)),
            ],
            compiler_params=pltpu.CompilerParams(
                collective_id=0, has_side_effects=True, vmem_limit_bytes=40 << 20
            ),
        )(
            science,
            template,
            sources.T,
            offsets,
            weights,
            valid,
            basis,
            coefs,
            background,
        )

    in_specs = (
        P("det", "row", None),
        P("det", None, "row", None),
        P(),
        P(None, "det", None),
        P(None, "det", None),
        P("det", None),
        P(),
        P("det", None),
        P("det"),
    )
    out_specs = P("det", None, "row", None)
    return jax.shard_map(body, mesh=mesh, in_specs=in_specs, out_specs=out_specs, check_vma=False)
```

time: 114 us -> 36.1 us (0.32); the launches traced: 112 us -> 35.8 us
  local copies, waits for them, and re-layouts: 39.3 us -> 4.78 us
  Pallas kernels: 0 us -> 30.3 us
  starting transfers between devices: 29.9 us -> 0 us
  matrix products: 23 us -> 0 us
  waiting for transfers between devices: 11 us -> 0 us
  other arithmetic: 5.43 us -> 0 us
  loops' own time: 1.73 us -> 0 us
    dynamic_slice x62 -> x0, local copies, waits for them, and re-layouts: 31 us -> none  [the longest x31 28.6 us: kernel_row(): lax.dynamic_index_in_dim(trail_bands, tap_row, 0, keepdims=False)]
    pallas_call x0 -> x1, Pallas kernels: none -> 30.3 us  [body(): pl.pallas_call(functools.partial(kernel, det_count, row_count), out_shape...]
    ppermute x8 -> x0, starting transfers between devices: 29.9 us -> none  [the longest x6 24.7 us: shifted(): return lax.ppermute(value, axis, pairs)]
    dot_general x81 -> x0, matrix products: 23 us -> none  [the longest x31 7.22 us: kernel_row(): jnp.einsum('ycj,ji->yci', main_part, lead_now, precision=highest)]
    ppermute x8 -> x0, waiting for transfers between devices: 11 us -> none  [the longest x6 11 us: shifted(): return lax.ppermute(value, axis, pairs)]
    slice x40 -> x0, local copies, waits for them, and re-layouts: 4.05 us -> none  [the longest x31 3.2 us: kernel_row(): rows_here[:, tile_size:].reshape(band_rows, tile_count, tile_size)]
    unnamed x17, local copies, waits for them, and re-layouts: 1.32 us -> 4.78 us
    another operation x1 -> x0, loops' own time: 1.73 us -> none  [body(): lax.fori_loop(0, kernel_width, kernel_row, jnp.zeros((band_rows, tile_cou...]
  transfers between devices with their start and end apart: 8 -> 0, of which waited for: 3 -> 0; matrix products, arithmetic and copies ran while one was open for 12% -> 0% of each run, Pallas kernels for 0% -> 0%
where the time goes in v1:
time: 36.1 us; the launch traced here: 35.8 us
  Pallas kernels  30.3 us (84%)
  local copies, waits for them, and re-layouts  4.78 us (13%)
  between operations  0.73 us (2%)
    pallas_call x1, Pallas kernels, body(): pl.pallas_call(functools.partial(kernel, det_count, row_count), out_shape...  30.3 us
    unnamed x17, local copies, waits for them, and re-layouts  4.78 us

profile of v1, /device:TPU:1, one launch (start us, length us, event | category | flops | bytes accessed | tf_op | source)
XLA Modules:
  0.0 35.8 jit_solution(366758764891831029)
XLA Ops:
  0.0 0.0 copy-start.5
  0.0 0.0 copy-start.7
  0.7 0.0 copy-start.4
  0.7 0.0 copy-start.6
  0.7 0.0 copy-done.5
  0.7 0.0 copy-done.7
  0.7 0.6 %copy-done.4 = s32[2,1,6]{2,1,0:T(1,128)S(1)} copy-done((s32[2,1,6]{2,1,0:T(1,128)S(1)}, s32[2,1,6]{2,1,0:T(1,128)}, u32[]{:S(2)}) %copy-start.4) | copy-done | bytes 72
  1.4 0.0 copy-done.6
  1.4 0.0 copy-start
  1.4 1.0 %copy-done = f32[27,31,31]{2,1,0:T(8,128)S(1)} copy-done((f32[27,31,31]{2,1,0:T(8,128)S(1)}, f32[27,31,31]{2,1,0:T(8,128)}, u32[]{:S(2)}) %copy-start) | copy-done | bytes 103812
  2.4 0.0 copy-start.1
  2.4 0.9 %copy-done.1 = f32[1,32,768]{2,1,0:T(8,128)S(1)} copy-done((f32[1,32,768]{2,1,0:T(8,128)S(1)}, f32[1,32,768]{2,1,0:T(8,128)}, u32[]{:S(2)}) %copy-start.1) | copy-done | bytes 98328
  3.3 0.0 copy-start.2
  3.3 0.9 %copy-done.2 = f32[1,6,32,128]{3,2,1,0:T(8,128)S(1)} copy-done((f32[1,6,32,128]{3,2,1,0:T(8,128)S(1)}, f32[1,6,32,128]{3,2,1,0:T(8,128)}, u32[]{:S(2)}) %copy-start.2) | copy-done | bytes 98328
  4.2 0.0 copy-start.3
  4.2 0.7 %copy-done.3 = s32[128,6]{0,1:T(8,128)S(1)} copy-done((s32[128,6]{0,1:T(8,128)S(1)}, s32[128,6]{0,1:T(8,128)}, u32[]{:S(2)}) %copy-start.3) | copy-done | bytes 3096
  4.9 30.3 %shard_map.91 = f32[1,6,32,128]{3,2,1,0:T(8,128)S(1)} custom-call(f32[1,32,768]{2,1,0:T(8,128)S(1)} %copy-done.1, f32[1,6,32,128]{3,2,1,0:T(8,128)S(1)} %copy-done.2, s32[6,128]{1,0:T(8,128)S(1)} %bitcast.1, s32[2,1,6]{2,1,0:T(1,128)S(1)} %copy-done.4, f32[2,1,6]{2,1,0:T(1,128)S(1)} %copy-done.5, s32[1,6]{1,0:T(1,128)S(1)} %copy-done.6, ...), custom_call_target="tpu_custom_call" | custom-call | tf_op jit(solution)/shard_map/pallas_call | solution.py:318
  35.2 0.6 %copy.12 = f32[1,6,32,128]{3,2,1,0:T(8,128)} copy(f32[1,6,32,128]{3,2,1,0:T(8,128)S(1)} %shard_map.91) | data formatting | bytes 196608
Async XLA Ops:
  0.0 0.7 %copy-start.5 = (f32[2,1,6]{2,1,0:T(1,128)S(1)}, f32[2,1,6]{2,1,0:T(1,128)}, u32[]{:S(2)}) copy-start(f32[2,1,6]{2,1,0:T(1,128)} %weights.1) | copy-start | bytes 148
  0.0 0.7 %copy-start.7 = (f32[1,27]{1,0:T(1,128)S(1)}, f32[1,27]{1,0:T(1,128)}, u32[]{:S(2)}) copy-start(f32[1,27]{1,0:T(1,128)} %coefs.1) | copy-start | bytes 328
  0.7 0.7 %copy-start.4 = (s32[2,1,6]{2,1,0:T(1,128)S(1)}, s32[2,1,6]{2,1,0:T(1,128)}, u32[]{:S(2)}) copy-start(s32[2,1,6]{2,1,0:T(1,128)} %offsets.1) | copy-start | bytes 148
  0.7 0.7 %copy-start.6 = (s32[1,6]{1,0:T(1,128)S(1)}, s32[1,6]{1,0:T(1,128)}, u32[]{:S(2)}) copy-start(s32[1,6]{1,0:T(1,128)} %valid.1) | copy-start | bytes 76
  1.4 1.0 %copy-start = (f32[27,31,31]{2,1,0:T(8,128)S(1)}, f32[27,31,31]{2,1,0:T(8,128)}, u32[]{:S(2)}) copy-start(f32[27,31,31]{2,1,0:T(8,128)} %basis.1) | copy-start | bytes 311368
  2.4 0.9 %copy-start.1 = (f32[1,32,768]{2,1,0:T(8,128)S(1)}, f32[1,32,768]{2,1,0:T(8,128)}, u32[]{:S(2)}) copy-start(f32[1,32,768]{2,1,0:T(8,128)} %science.1) | copy-start | bytes 294916
  3.3 0.9 %copy-start.2 = (f32[1,6,32,128]{3,2,1,0:T(8,128)S(1)}, f32[1,6,32,128]{3,2,1,0:T(8,128)}, u32[]{:S(2)}) copy-start(f32[1,6,32,128]{3,2,1,0:T(8,128)} %template.1) | copy-start | bytes 294916
  4.2 0.7 %copy-start.3 = (s32[128,6]{0,1:T(8,128)S(1)}, s32[128,6]{0,1:T(8,128)}, u32[]{:S(2)}) copy-start(s32[128,6]{0,1:T(8,128)} %param.11) | copy-start | bytes 9220

commit v2 on v1

v2 whole, which is shorter than its diff:
```python
import functools

import jax
import jax.numpy as jnp
from jax import lax
from jax.experimental import pallas as pl
from jax.experimental.pallas import tpu as pltpu
from jax.sharding import PartitionSpec as P

MESH = pl.DeviceIdType.MESH
SPAN = 4
CAP = 3
TILES = 6
TILE = 128
BAND = 32
ABOVE = 16
BELOW = 24
DEEP = ABOVE + BAND + BELOW
KW = 31
HALF = 15
NB = 27
GROUP = 8
MAXOFF = 4
STRIP = 32
LEFT, RIGHT, ZERO_TILE = 6, 7, 8


def split(x):
    high = x.astype(jnp.bfloat16).astype(jnp.float32)
    return high, x - high


def kernel(
    det_count,
    row_count,
    science,
    template,
    sources,
    offsets,
    weights,
    valid,
    basis,
    coefs,
    background,
    out,
    tally_out,
    own,
    tiles,
    edges,
    images,
    seen,
    bands_even,
    bands_odd,
    basis_v,
    model_v,
    taps,
    taps_back,
    floats,
    ints,
    float_s,
    int_s,
    sources_s,
    offsets_s,
    weights_s,
    valid_s,
    coefs_s,
    local_sem,
    send_sem,
    recv_sem,
):
    p = lax.axis_index("det")
    r = lax.axis_index("row")

    def det(j):
        return lax.rem(p + (j + det_count), det_count)

    def row(j):
        return lax.rem(r + (j + row_count), row_count)

    peers = [(det(j), r) for j in (1, -1, 2, -2, 3, -3)]
    peers += [(p, row(1)), (p, row(-1))]
    peers += [(det(j), row(i)) for j in (1, -1) for i in (1, -1)]
    barrier = pltpu.get_barrier_semaphore()
    for peer in peers:
        pl.semaphore_signal(barrier, inc=1, device_id=peer, device_id_type=MESH)

    load_own = pltpu.make_async_copy(template.at[0], own, local_sem.at[0])
    load_tiles = pltpu.make_async_copy(
        template.at[0], tiles.at[pl.ds(0, TILES), pl.ds(ABOVE, BAND), :], local_sem.at[1]
    )
    load_seen = pltpu.make_async_copy(
        science.at[0, :, pl.ds(0, CAP * TILE)], seen.at[0], local_sem.at[2]
    )
    load_basis = pltpu.make_async_copy(basis, basis_v, local_sem.at[5])
    small = []
    for i, (src, dst) in enumerate(
        (
            (sources, sources_s),
            (offsets, offsets_s),
            (weights, weights_s),
            (valid, valid_s),
            (coefs, coefs_s),
        )
    ):
        small.append(pltpu.make_async_copy(src, dst, local_sem.at[6 + i]))
    load_own.start()
    for copy in small:
        copy.start()
    load_basis.start()
    load_tiles.start()
    load_seen.start()
    for copy in small:
        copy.wait()

    runs = []
    for q in range(SPAN):
        d = det(-q)
        start = jnp.int32(0)
        length = jnp.int32(0)
        for c in range(TILES):
            reach = lax.rem(sources_s[c, d] // TILES - d + det_count, det_count)
            start = start + jnp.where(reach < q, 1, 0)
            length = length + jnp.where(reach == q, 1, 0)
        start = jnp.clip(start, 0, TILES - 1)
        first = jnp.clip(sources_s[start, d] - p * TILES, 0, TILES - 1)
        runs.append((start, length, first))

    lane = lax.broadcasted_iota(jnp.int32, (1, TILE), 1)
    packed = jnp.zeros((1, TILE), jnp.float32)
    whole = jnp.zeros((1, TILE), jnp.int32)
    for k in range(NB):
        packed = jnp.where(lane == k, coefs_s[0, k], packed)
    packed = jnp.where(lane == NB, background[0], packed)
    for c in range(TILES):
        packed = jnp.where(lane == 28 + c, weights_s[0, 0, c], packed)
        packed = jnp.where(lane == 34 + c, weights_s[1, 0, c], packed)
        whole = jnp.where(lane == c, offsets_s[0, 0, c], whole)
        whole = jnp.where(lane == 6 + c, offsets_s[1, 0, c], whole)
        whole = jnp.where(lane == 12 + c, valid_s[0, c], whole)
    floats[0] = packed
    ints[0] = whole

    tiles[ZERO_TILE] = jnp.zeros((DEEP, TILE), jnp.float32)
    load_own.wait()
    strip = lax.broadcasted_iota(jnp.int32, (BAND, TILE), 1) // STRIP
    ends = jnp.zeros((BAND, TILE), jnp.float32)
    begins = jnp.zeros((BAND, TILE), jnp.float32)
    for j in range(CAP):
        start, length, first = runs[j]
        last = own[jnp.clip(first + length - 1, 0, TILES - 1)]
        ends = jnp.where(strip == j, pltpu.roll(last, STRIP * (j + 1), 1), ends)
        start, length, first = runs[j + 1]
        head = own[first]
        begins = jnp.where(strip == j, pltpu.roll(head, STRIP * j, 1) if j else head, begins)
    edges[0] = ends
    edges[1] = begins

    load_tiles.wait()
    pl.semaphore_wait(barrier, len(peers))

    copies = []

    def send(src, dst, peer):
        i = len(copies)
        copy = pltpu.make_async_remote_copy(
            src_ref=src,
            dst_ref=dst,
            send_sem=send_sem.at[i],
            recv_sem=recv_sem.at[i],
            device_id=peer,
            device_id_type=MESH,
        )
        copy.start()
        copies.append(copy)

    low_rows, high_rows = pl.ds(0, ABOVE), pl.ds(ABOVE + BAND, BELOW)
    send(own.at[:, pl.ds(0, BELOW), :], tiles.at[pl.ds(0, TILES), high_rows, :], (p, row(-1)))
    send(
        own.at[:, pl.ds(BAND - ABOVE, ABOVE), :],
        tiles.at[pl.ds(0, TILES), low_rows, :],
        (p, row(1)),
    )
    for j in range(1, SPAN):
        send(floats.at[0], floats.at[j], (det(j), r))
        send(ints.at[0], ints.at[j], (det(j), r))
    for side, j, at in ((0, 1, LEFT), (1, -1, RIGHT)):
        send(
            edges.at[side, pl.ds(0, BELOW), :], tiles.at[at, high_rows, :], (det(j), row(-1))
        )
        send(
            edges.at[side, pl.ds(BAND - ABOVE, ABOVE), :],
            tiles.at[at, low_rows, :],
            (det(j), row(1)),
        )
        send(edges.at[side], tiles.at[at, pl.ds(ABOVE, BAND), :], (det(j), r))
    for j in range(1, SPAN):
        send(
            science.at[0, :, pl.ds(j * TILE, CAP * TILE)],
            seen.at[j],
            (det(j), r),
        )

    sub = lax.broadcasted_iota(jnp.int32, (8, TILE), 0)
    across = lax.broadcasted_iota(jnp.int32, (8, TILE), 1)

    def mirrored(q, coefficient):
        total = coefficient(0) * basis_v[0]
        for k in range(1, NB):
            total = total + coefficient(k) * basis_v[k]
        taps[pl.ds(0, KW), pl.ds(0, KW)] = total
        high, low = split(taps[...])
        both = jnp.dot(
            jnp.concatenate([high, low], axis=0), mirror, preferred_element_type=jnp.float32
        )
        taps_back[q] = both[:BAND] + both[BAND:]

    def toeplitz(q, a, bands, place):
        line = jnp.broadcast_to(taps_back[q, pl.ds(a, 1), :], (8, TILE))
        block = pltpu.roll(line, 0, 1, stride=1, stride_axis=0)
        for jb in range(TILE // 8):
            high, low = split(block if jb == 0 else pltpu.roll(block, 8 * jb, 1))
            if jb < BAND // 8:
                lead = across <= sub + 8 * jb
                at = pl.ds(TILE + 8 * jb, 8)
                bands[place, a, at, pl.ds(0, TILE)] = jnp.where(lead, 0.0, high)
                bands[place, a, at, pl.ds(TILE, TILE)] = jnp.where(lead, 0.0, low)
                high, low = jnp.where(lead, high, 0.0), jnp.where(lead, low, 0.0)
            bands[place, a, pl.ds(8 * jb, 8), pl.ds(0, TILE)] = high
            bands[place, a, pl.ds(8 * jb, 8), pl.ds(TILE, TILE)] = low

    def toeplitz_first_pair(q):
        def group(step, carry):
            for k in range(GROUP):
                toeplitz(q, step * GROUP + k, bands_even, q)
            return carry

        lax.fori_loop(0, BAND // GROUP, group, 0)

    rows128 = lax.broadcasted_iota(jnp.int32, (TILE, TILE), 0)
    cols128 = lax.broadcasted_iota(jnp.int32, (TILE, TILE), 1)
    mirror = jnp.where(lax.rem(rows128 + cols128, TILE) == 0, 1.0, 0.0).astype(jnp.float32)
    taps[...] = jnp.zeros((BAND, TILE), jnp.float32)
    load_basis.wait()
    mirrored(0, lambda k: coefs_s[0, k])
    toeplitz_first_pair(0)
    for copy in copies[2:8]:
        copy.wait_recv()
    to_float = pltpu.make_async_copy(floats, float_s, local_sem.at[3])
    to_int = pltpu.make_async_copy(ints, int_s, local_sem.at[4])
    to_float.start()
    to_int.start()
    to_float.wait()
    to_int.wait()
    for q in range(1, SPAN):
        mirrored(q, lambda k, q=q: float_s[q, 0, k])
    toeplitz_first_pair(1)
    for copy in copies[:2] + copies[8:14]:
        copy.wait_recv()

    eight = lax.broadcasted_iota(jnp.int32, (2 * BAND, TILE), 0)
    wide = lax.broadcasted_iota(jnp.int32, (2 * BAND, TILE), 1)
    line_at = eight + (r * BAND - HALF)
    tail = wide < HALF
    for q in range(SPAN):
        start, length, first = runs[q]
        before = None
        for m in range(CAP + 2):
            c = jnp.clip(start + (m - 1), 0, TILES - 1)
            row_shift = jnp.clip(int_s[q, 0, c], 0, MAXOFF - 1)
            col_shift = int_s[q, 0, 6 + c]
            row_weight, col_weight = float_s[q, 0, 28 + c], float_s[q, 0, 34 + c]
            turn = jnp.int32(HALF + TILE) - col_shift
            last_lane = TILE - 1
            if m == 0:
                index = LEFT if q > 0 else ZERO_TILE
                last_lane = STRIP * q - 1 if q > 0 else TILE - 1
                turn = turn - STRIP * q
            else:
                edge = RIGHT if q < SPAN - 1 else ZERO_TILE
                index = jnp.where(
                    m <= length, first + (m - 1), jnp.where(m == length + 1, edge, ZERO_TILE)
                )
                index = jnp.clip(index, 0, ZERO_TILE)
                if q > 0:
                    turn = turn - jnp.where(m > length, STRIP * q, 0)
            upper = tiles[index, pl.ds(1 + row_shift, 2 * BAND), :]
            lower = tiles[index, pl.ds(2 + row_shift, 2 * BAND), :]
            limit = row_count * BAND - row_shift
            upper = jnp.where(line_at < limit, (1.0 - row_weight) * upper, 0.0)
            lower = jnp.where(line_at < limit - 1, row_weight * lower, 0.0)
            mixed = jnp.where(line_at >= 0, upper + lower, 0.0)
            last = jnp.broadcast_to(mixed[:, last_lane : last_lane + 1], (2 * BAND, TILE))
            left = pltpu.roll(mixed, lax.rem(turn, TILE), 1)
            left = jnp.where(tail & (wide > HALF - 1 - col_shift), last, left)
            following = pltpu.roll(mixed, lax.rem(turn - 1, TILE), 1)
            following = jnp.where(tail & (wide > HALF - 2 - col_shift), last, following)
            now = (1.0 - col_weight) * left + col_weight * following
            if m > 0:
                high, low = split(jnp.where(tail, before, now))
                images[q, 0, m - 1] = high
                images[q, 1, m - 1] = low
            before = now

    rest = jnp.zeros((TILE - BAND, 2 * TILE), jnp.float32)
    model_v[...] = jnp.zeros_like(model_v)

    def convolve(pair, bands):
        def group(step, carry):
            base = step * GROUP
            for i in range(2):
                q = 2 * pair + i
                if pair == 0:
                    for k in range(GROUP):
                        toeplitz(q + 2, base + k, bands_odd, i)
                total = None
                for k in range(GROUP):
                    blocks = []
                    for part in range(2):
                        views = [
                            images[q, part, t, pl.ds(base + k, BAND), :] for t in range(CAP + 1)
                        ]
                        blocks += [
                            jnp.concatenate([views[t], views[t + 1]], axis=1)
                            for t in range(CAP)
                        ]
                    band = jnp.concatenate([bands[i, base + k], rest], axis=0)
                    term = jnp.dot(
                        jnp.concatenate(blocks, axis=0), band, preferred_element_type=jnp.float32
                    )
                    total = term if total is None else total + term
                model_v[q] += total
            return carry

        lax.fori_loop(0, BAND // GROUP, group, 0)

    convolve(0, bands_even)
    convolve(1, bands_odd)

    load_seen.wait()
    for copy in copies[14:]:
        copy.wait_recv()

    down = lax.broadcasted_iota(jnp.int32, (BAND, TILE), 0) + r * BAND
    parts = []
    for q in range(SPAN):
        start, length, first = runs[q]
        for k in range(CAP):
            acc = model_v[q]
            at = k * BAND
            model = acc[at : at + BAND, :TILE] + acc[at : at + BAND, TILE:]
            at += CAP * BAND
            model = model + (acc[at : at + BAND, :TILE] + acc[at : at + BAND, TILE:])
            pixels = seen[q, :, pl.ds(k * TILE, TILE)]
            if k == 0 and q > 0:
                pixels = jnp.where(start == q, pixels, seen[q, :, pl.ds(2 * TILE, TILE)])
            c = jnp.clip(start + k, 0, TILES - 1)
            residual = jnp.where(
                down < int_s[q, 0, 12 + c], pixels - model - float_s[q, 0, NB], 0.0
            )
            parts.append((jnp.where(k < length, first + k, -1), residual))
    for s in range(TILES):
        total = jnp.zeros((BAND, TILE), jnp.float32)
        tally = jnp.float32(0.0)
        for slot, residual in parts:
            total = total + jnp.where(slot == s, residual, 0.0)
            tally = tally + jnp.where(slot == s, 1.0, 0.0)
        out[0, s] = total
        tally_out[0, s] = jnp.full((BAND, TILE), jnp.maximum(tally, 1.0), jnp.float32)

    for copy in copies:
        copy.wait_send()


def solution(mesh):
    det_count, row_count = mesh.shape["det"], mesh.shape["row"]

    def body(
        science, template, sources, offsets, weights, valid, basis, coefs, background
    ):
        vmem = pl.BlockSpec(memory_space=pltpu.VMEM)
        hbm = pl.BlockSpec(memory_space=pltpu.HBM)
        total, tally = pl.pallas_call(
            functools.partial(kernel, det_count, row_count),
            out_shape=(
                jax.ShapeDtypeStruct(template.shape, jnp.float32),
                jax.ShapeDtypeStruct(template.shape, jnp.float32),
            ),
            in_specs=[hbm] * 8 + [pl.BlockSpec(memory_space=pltpu.SMEM)],
            out_specs=(vmem, vmem),
            scratch_shapes=[
                pltpu.VMEM((TILES, BAND, TILE), jnp.float32),
                pltpu.VMEM((ZERO_TILE + 1, DEEP, TILE), jnp.float32),
                pltpu.VMEM((2, BAND, TILE), jnp.float32),
                pltpu.VMEM((SPAN, 2, CAP + 1, 2 * BAND, TILE), jnp.float32),
                pltpu.VMEM((SPAN, BAND, CAP * TILE), jnp.float32),
                pltpu.VMEM((2, BAND, TILE + BAND, 2 * TILE), jnp.float32),
                pltpu.VMEM((2, BAND, TILE + BAND, 2 * TILE), jnp.float32),
                pltpu.VMEM((NB, KW, KW), jnp.float32),
                pltpu.VMEM((SPAN, 2 * CAP * BAND, 2 * TILE), jnp.float32),
                pltpu.VMEM((BAND, TILE), jnp.float32),
                pltpu.VMEM((SPAN, BAND, TILE), jnp.float32),
                pltpu.VMEM((SPAN, 1, TILE), jnp.float32),
                pltpu.VMEM((SPAN, 1, TILE), jnp.int32),
                pltpu.SMEM((SPAN, 1, TILE), jnp.float32),
                pltpu.SMEM((SPAN, 1, TILE), jnp.int32),
                pltpu.SMEM((TILES, TILE), jnp.int32),
                pltpu.SMEM((2, 1, TILES), jnp.int32),
                pltpu.SMEM((2, 1, TILES), jnp.float32),
                pltpu.SMEM((1, TILES), jnp.int32),
                pltpu.SMEM((1, NB), jnp.float32),
                pltpu.SemaphoreType.DMA((11,)),
                pltpu.SemaphoreType.DMA((17,)),
                pltpu.SemaphoreType.DMA((17,)),
            ],
            compiler_params=pltpu.CompilerParams(
                collective_id=0, has_side_effects=True, vmem_limit_bytes=54 << 20
            ),
        )(
            science,
            template,
            sources.T,
            offsets,
            weights,
            valid,
            basis,
            coefs,
            background,
        )
        return total / tally

    in_specs = (
        P("det", "row", None),
        P("det", None, "row", None),
        P(),
        P(None, "det", None),
        P(None, "det", None),
        P("det", None),
        P(),
        P("det", None),
        P("det"),
    )
    out_specs = P("det", None, "row", None)
    return jax.shard_map(body, mesh=mesh, in_specs=in_specs, out_specs=out_specs, check_vma=False)
```

time: 36.1 us -> 30.7 us (0.85)
  local copies, waits for them, and re-layouts: 4.78 us -> 0 us
  Pallas kernels: 30.3 us -> 28.3 us
  other arithmetic: 0 us -> 1.6 us
    unnamed x17 -> x0, local copies, waits for them, and re-layouts: 4.78 us -> none
    pallas_call x1, Pallas kernels: 30.3 us -> 28.3 us  [body(): pl.pallas_call(functools.partial(kernel, det_count, row_count), out_shape...]
    div x0 -> x1, other arithmetic: none -> 1.6 us  [body(): return total / tally]
where the time goes in v2:
time: 30.7 us; the launch traced here: 30.6 us
  Pallas kernels  28.3 us (92%)
  other arithmetic  1.6 us (5%)
  between operations  0.66 us (2%)
    pallas_call x1, Pallas kernels, body(): pl.pallas_call(functools.partial(kernel, det_count, row_count), out_shape...  28.3 us
    div x1, other arithmetic, body(): return total / tally  1.6 us

profile of v2, /device:TPU:1, one launch (start us, length us, event | category | flops | bytes accessed | tf_op | source)
XLA Modules:
  0.0 30.6 jit_solution(3889985857800013614)
XLA Ops:
  0.7 28.3 %shard_map.91 = (f32[1,6,32,128]{3,2,1,0:T(8,128)}, f32[1,6,32,128]{3,2,1,0:T(8,128)}) custom-call(f32[1,32,768]{2,1,0:T(8,128)} %science.1, f32[1,6,32,128]{3,2,1,0:T(8,128)} %template.1, s32[6,128]{1,0:T(8,128)} %bitcast.1, s32[2,1,6]{2,1,0:T(1,128)} %offsets.1, f32[2,1,6]{2,1,0:T(1,128)} %weights.1, s32[1,6]{1,0:T(1,128)} %valid.1, f32[27,31,31]{2,1,0:T(8,128)} %basis.1, ...), custom_call_target="tpu_custom_call" | custom-call | tf_op jit(solution)/shard_map/pallas_call | solution.py:382
  29.0 1.6 %div.3 = f32[1,6,32,128]{3,2,1,0:T(8,128)} divide(f32[1,6,32,128]{3,2,1,0:T(8,128)} %get-tuple-element.7, f32[1,6,32,128]{3,2,1,0:T(8,128)} %get-tuple-element.8) | non-fusion elementwise | flops 24576 | bytes 294912 | tf_op jit(solution)/shard_map/div | solution.py:429

commit v3 on v2

--- a/solution.py
+++ b/solution.py
@@ -20,6 +20,7 @@
 HALF = 15
 NB = 27
 GROUP = 8
+DOTS = 32
 MAXOFF = 4
 STRIP = 32
 LEFT, RIGHT, ZERO_TILE = 6, 7, 8
@@ -112,19 +113,6 @@
     for copy in small:
         copy.wait()
 
-    runs = []
-    for q in range(SPAN):
-        d = det(-q)
-        start = jnp.int32(0)
-        length = jnp.int32(0)
-        for c in range(TILES):
-            reach = lax.rem(sources_s[c, d] // TILES - d + det_count, det_count)
-            start = start + jnp.where(reach < q, 1, 0)
-            length = length + jnp.where(reach == q, 1, 0)
-        start = jnp.clip(start, 0, TILES - 1)
-        first = jnp.clip(sources_s[start, d] - p * TILES, 0, TILES - 1)
-        runs.append((start, length, first))
-
     lane = lax.broadcasted_iota(jnp.int32, (1, TILE), 1)
     packed = jnp.zeros((1, TILE), jnp.float32)
     whole = jnp.zeros((1, TILE), jnp.int32)
@@ -140,8 +128,49 @@
     floats[0] = packed
     ints[0] = whole
 
+    load_own.wait()
+    pl.semaphore_wait(barrier, len(peers))
+
+    copies = []
+
+    def send(src, dst, peer):
+        i = len(copies)
+        copy = pltpu.make_async_remote_copy(
+            src_ref=src,
+            dst_ref=dst,
+            send_sem=send_sem.at[i],
+            recv_sem=recv_sem.at[i],
+            device_id=peer,
+            device_id_type=MESH,
+        )
+        copy.start()
+        copies.append(copy)
+
+    low_rows, high_rows = pl.ds(0, ABOVE), pl.ds(ABOVE + BAND, BELOW)
+    send(own.at[:, pl.ds(0, BELOW), :], tiles.at[pl.ds(0, TILES), high_rows, :], (p, row(-1)))
+    send(
+        own.at[:, pl.ds(BAND - ABOVE, ABOVE), :],
+        tiles.at[pl.ds(0, TILES), low_rows, :],
+        (p, row(1)),
+    )
+    for j in range(1, SPAN):
+        send(floats.at[0], floats.at[j], (det(j), r))
+        send(ints.at[0], ints.at[j], (det(j), r))
+
+    runs = []
+    for q in range(SPAN):
+        d = det(-q)
+        start = jnp.int32(0)
+        length = jnp.int32(0)
+        for c in range(TILES):
+            reach = lax.rem(sources_s[c, d] // TILES - d + det_count, det_count)
+            start = start + jnp.where(reach < q, 1, 0)
+            length = length + jnp.where(reach == q, 1, 0)
+        start = jnp.clip(start, 0, TILES - 1)
+        first = jnp.clip(sources_s[start, d] - p * TILES, 0, TILES - 1)
+        runs.append((start, length, first))
+
     tiles[ZERO_TILE] = jnp.zeros((DEEP, TILE), jnp.float32)
-    load_own.wait()
     strip = lax.broadcasted_iota(jnp.int32, (BAND, TILE), 1) // STRIP
     ends = jnp.zeros((BAND, TILE), jnp.float32)
     begins = jnp.zeros((BAND, TILE), jnp.float32)
@@ -155,34 +184,6 @@
     edges[0] = ends
     edges[1] = begins
 
-    load_tiles.wait()
-    pl.semaphore_wait(barrier, len(peers))
-
-    copies = []
-
-    def send(src, dst, peer):
-        i = len(copies)
-        copy = pltpu.make_async_remote_copy(
-            src_ref=src,
-            dst_ref=dst,
-            send_sem=send_sem.at[i],
-            recv_sem=recv_sem.at[i],
-            device_id=peer,
-            device_id_type=MESH,
-        )
-        copy.start()
-        copies.append(copy)
-
-    low_rows, high_rows = pl.ds(0, ABOVE), pl.ds(ABOVE + BAND, BELOW)
-    send(own.at[:, pl.ds(0, BELOW), :], tiles.at[pl.ds(0, TILES), high_rows, :], (p, row(-1)))
-    send(
-        own.at[:, pl.ds(BAND - ABOVE, ABOVE), :],
-        tiles.at[pl.ds(0, TILES), low_rows, :],
-        (p, row(1)),
-    )
-    for j in range(1, SPAN):
-        send(floats.at[0], floats.at[j], (det(j), r))
-        send(ints.at[0], ints.at[j], (det(j), r))
     for side, j, at in ((0, 1, LEFT), (1, -1, RIGHT)):
         send(
             edges.at[side, pl.ds(0, BELOW), :], tiles.at[at, high_rows, :], (det(j), row(-1))
@@ -254,6 +255,7 @@
     for q in range(1, SPAN):
         mirrored(q, lambda k, q=q: float_s[q, 0, k])
     toeplitz_first_pair(1)
+    load_tiles.wait()
     for copy in copies[:2] + copies[8:14]:
         copy.wait_recv()
 
@@ -306,14 +308,14 @@
 
     def convolve(pair, bands):
         def group(step, carry):
-            base = step * GROUP
+            base = step * DOTS
             for i in range(2):
                 q = 2 * pair + i
                 if pair == 0:
-                    for k in range(GROUP):
+                    for k in range(DOTS):
                         toeplitz(q + 2, base + k, bands_odd, i)
                 total = None
-                for k in range(GROUP):
+                for k in range(DOTS):
                     blocks = []
                     for part in range(2):
                         views = [
@@ -331,7 +333,7 @@
                 model_v[q] += total
             return carry
 
-        lax.fori_loop(0, BAND // GROUP, group, 0)
+        lax.fori_loop(0, BAND // DOTS, group, 0)
 
     convolve(0, bands_even)
     convolve(1, bands_odd)

time: 30.7 us -> 27.8 us (0.906)
  Pallas kernels: 28.3 us -> 25.4 us
    pallas_call x1, Pallas kernels: 28.3 us -> 25.4 us  [body(): pl.pallas_call(functools.partial(kernel, det_count, row_count), out_shape...]
where the time goes in v3:
time: 27.8 us; the launch traced here: 27.7 us
  Pallas kernels  25.4 us (91%)
  other arithmetic  1.6 us (6%)
  between operations  0.66 us (2%)
    pallas_call x1, Pallas kernels, body(): pl.pallas_call(functools.partial(kernel, det_count, row_count), out_shape...  25.4 us
    div x1, other arithmetic, body(): return total / tally  1.6 us

profile of v3, /device:TPU:1, one launch (start us, length us, event | category | flops | bytes accessed | tf_op | source)
XLA Modules:
  0.0 27.7 jit_solution(11842017039304671277)
XLA Ops:
  0.7 25.4 %shard_map.91 = (f32[1,6,32,128]{3,2,1,0:T(8,128)}, f32[1,6,32,128]{3,2,1,0:T(8,128)}) custom-call(f32[1,32,768]{2,1,0:T(8,128)} %science.1, f32[1,6,32,128]{3,2,1,0:T(8,128)} %template.1, s32[6,128]{1,0:T(8,128)} %bitcast.1, s32[2,1,6]{2,1,0:T(1,128)} %offsets.1, f32[2,1,6]{2,1,0:T(1,128)} %weights.1, s32[1,6]{1,0:T(1,128)} %valid.1, f32[27,31,31]{2,1,0:T(8,128)} %basis.1, ...), custom_call_target="tpu_custom_call" | custom-call | tf_op jit(solution)/shard_map/pallas_call | solution.py:384
  26.1 1.6 %div.3 = f32[1,6,32,128]{3,2,1,0:T(8,128)} divide(f32[1,6,32,128]{3,2,1,0:T(8,128)} %get-tuple-element.7, f32[1,6,32,128]{3,2,1,0:T(8,128)} %get-tuple-element.8) | non-fusion elementwise | flops 24576 | bytes 294912 | tf_op jit(solution)/shard_map/div | solution.py:431

commit v4 on v3

--- a/solution.py
+++ b/solution.py
@@ -22,6 +22,7 @@
 GROUP = 8
 DOTS = 32
 MAXOFF = 4
+STEP = 96
 STRIP = 32
 LEFT, RIGHT, ZERO_TILE = 6, 7, 8
 
@@ -201,8 +202,6 @@
             (det(j), r),
         )
 
-    sub = lax.broadcasted_iota(jnp.int32, (8, TILE), 0)
-    across = lax.broadcasted_iota(jnp.int32, (8, TILE), 1)
 
     def mirrored(q, coefficient):
         total = coefficient(0) * basis_v[0]
@@ -218,16 +217,18 @@
     def toeplitz(q, a, bands, place):
         line = jnp.broadcast_to(taps_back[q, pl.ds(a, 1), :], (8, TILE))
         block = pltpu.roll(line, 0, 1, stride=1, stride_axis=0)
-        for jb in range(TILE // 8):
-            high, low = split(block if jb == 0 else pltpu.roll(block, 8 * jb, 1))
-            if jb < BAND // 8:
-                lead = across <= sub + 8 * jb
-                at = pl.ds(TILE + 8 * jb, 8)
-                bands[place, a, at, pl.ds(0, TILE)] = jnp.where(lead, 0.0, high)
-                bands[place, a, at, pl.ds(TILE, TILE)] = jnp.where(lead, 0.0, low)
-                high, low = jnp.where(lead, high, 0.0), jnp.where(lead, low, 0.0)
-            bands[place, a, pl.ds(8 * jb, 8), pl.ds(0, TILE)] = high
-            bands[place, a, pl.ds(8 * jb, 8), pl.ds(TILE, TILE)] = low
+        for jb in range(TILE // 16):
+            turned = jnp.concatenate(
+                [
+                    block if shift == 0 else pltpu.roll(block, shift, 1)
+                    for shift in (16 * jb, 16 * jb + 8)
+                ],
+                axis=0,
+            )
+            high = turned.astype(jnp.bfloat16)
+            low = (turned - high.astype(jnp.float32)).astype(jnp.bfloat16)
+            bands[place, a, pl.ds(16 * jb, 16), pl.ds(0, TILE)] = high
+            bands[place, a, pl.ds(16 * jb, 16), pl.ds(TILE, TILE)] = low
 
     def toeplitz_first_pair(q):
         def group(step, carry):
@@ -265,7 +266,7 @@
     tail = wide < HALF
     for q in range(SPAN):
         start, length, first = runs[q]
-        before = None
+        before = former = None
         for m in range(CAP + 2):
             c = jnp.clip(start + (m - 1), 0, TILES - 1)
             row_shift = jnp.clip(int_s[q, 0, c], 0, MAXOFF - 1)
@@ -298,12 +299,20 @@
             following = jnp.where(tail & (wide > HALF - 2 - col_shift), last, following)
             now = (1.0 - col_weight) * left + col_weight * following
             if m > 0:
-                high, low = split(jnp.where(tail, before, now))
-                images[q, 0, m - 1] = high
-                images[q, 1, m - 1] = low
+                t = m - 1
+                here = jnp.where(tail, before, now)
+                window = here
+                if t > 0:
+                    skip = TILE - STEP
+                    window = jnp.where(wide >= TILE - skip * t, former, here)
+                    window = pltpu.roll(window, skip * t, 1)
+                high, low = split(window)
+                images[q, 0, t] = high
+                images[q, 1, t] = low
+                former = here
             before = now
 
-    rest = jnp.zeros((TILE - BAND, 2 * TILE), jnp.float32)
+    rest = jnp.zeros((TILE, TILE), jnp.bfloat16)
     model_v[...] = jnp.zeros_like(model_v)
 
     def convolve(pair, bands):
@@ -316,18 +325,19 @@
                         toeplitz(q + 2, base + k, bands_odd, i)
                 total = None
                 for k in range(DOTS):
-                    blocks = []
-                    for part in range(2):
-                        views = [
-                            images[q, part, t, pl.ds(base + k, BAND), :] for t in range(CAP + 1)
-                        ]
-                        blocks += [
-                            jnp.concatenate([views[t], views[t + 1]], axis=1)
-                            for t in range(CAP)
-                        ]
-                    band = jnp.concatenate([bands[i, base + k], rest], axis=0)
+                    blocks = [
+                        jnp.concatenate(
+                            [images[q, part, t, pl.ds(base + k, BAND), :] for part in range(2)],
+                            axis=1,
+                        )
+                        for t in range(CAP + 1)
+                    ]
+                    band = bands[i, base + k]
+                    lower = jnp.concatenate([band[:, :TILE], rest], axis=1)
                     term = jnp.dot(
-                        jnp.concatenate(blocks, axis=0), band, preferred_element_type=jnp.float32
+                        jnp.concatenate(blocks, axis=0).astype(jnp.bfloat16),
+                        jnp.concatenate([band, lower], axis=0),
+                        preferred_element_type=jnp.float32,
                     )
                     total = term if total is None else total + term
                 model_v[q] += total
@@ -343,15 +353,17 @@
         copy.wait_recv()
 
     down = lax.broadcasted_iota(jnp.int32, (BAND, TILE), 0) + r * BAND
+    column = lax.broadcasted_iota(jnp.int32, (BAND, TILE), 1)
     parts = []
     for q in range(SPAN):
         start, length, first = runs[q]
+        strips = []
+        for t in range(CAP + 1):
+            acc = model_v[q, pl.ds(t * BAND, BAND), :]
+            part = acc[:, :TILE] + acc[:, TILE:]
+            strips.append(pltpu.roll(part, TILE - (TILE - STEP) * t, 1) if t else part)
         for k in range(CAP):
-            acc = model_v[q]
-            at = k * BAND
-            model = acc[at : at + BAND, :TILE] + acc[at : at + BAND, TILE:]
-            at += CAP * BAND
-            model = model + (acc[at : at + BAND, :TILE] + acc[at : at + BAND, TILE:])
+            model = jnp.where(column < STEP - (TILE - STEP) * k, strips[k], strips[k + 1])
             pixels = seen[q, :, pl.ds(k * TILE, TILE)]
             if k == 0 and q > 0:
                 pixels = jnp.where(start == q, pixels, seen[q, :, pl.ds(2 * TILE, TILE)])
@@ -395,10 +407,10 @@
                 pltpu.VMEM((2, BAND, TILE), jnp.float32),
                 pltpu.VMEM((SPAN, 2, CAP + 1, 2 * BAND, TILE), jnp.float32),
                 pltpu.VMEM((SPAN, BAND, CAP * TILE), jnp.float32),
-                pltpu.VMEM((2, BAND, TILE + BAND, 2 * TILE), jnp.float32),
-                pltpu.VMEM((2, BAND, TILE + BAND, 2 * TILE), jnp.float32),
+                pltpu.VMEM((2, BAND, TILE, 2 * TILE), jnp.bfloat16),
+                pltpu.VMEM((2, BAND, TILE, 2 * TILE), jnp.bfloat16),
                 pltpu.VMEM((NB, KW, KW), jnp.float32),
-                pltpu.VMEM((SPAN, 2 * CAP * BAND, 2 * TILE), jnp.float32),
+                pltpu.VMEM((SPAN, (CAP + 1) * BAND, 2 * TILE), jnp.float32),
                 pltpu.VMEM((BAND, TILE), jnp.float32),
                 pltpu.VMEM((SPAN, BAND, TILE), jnp.float32),
                 pltpu.VMEM((SPAN, 1, TILE), jnp.float32),

time: 27.8 us -> 26.8 us (0.964)
  Pallas kernels: 25.4 us -> 24.4 us
    pallas_call x1, Pallas kernels: 25.4 us -> 24.4 us  [body(): pl.pallas_call(functools.partial(kernel, det_count, row_count), out_shape...]
where the time goes in v4:
time: 26.8 us; the launch traced here: 26.6 us
  Pallas kernels  24.4 us (91%)
  other arithmetic  1.6 us (6%)
  between operations  0.66 us (2%)
    pallas_call x1, Pallas kernels, body(): pl.pallas_call(functools.partial(kernel, det_count, row_count), out_shape...  24.4 us
    div x1, other arithmetic, body(): return total / tally  1.6 us

profile of v4, /device:TPU:1, one launch (start us, length us, event | category | flops | bytes accessed | tf_op | source)
XLA Modules:
  0.0 26.6 jit_solution(349675501754809812)
XLA Ops:
  0.7 24.4 %shard_map.91 = (f32[1,6,32,128]{3,2,1,0:T(8,128)}, f32[1,6,32,128]{3,2,1,0:T(8,128)}) custom-call(f32[1,32,768]{2,1,0:T(8,128)} %science.1, f32[1,6,32,128]{3,2,1,0:T(8,128)} %template.1, s32[6,128]{1,0:T(8,128)} %bitcast.1, s32[2,1,6]{2,1,0:T(1,128)} %offsets.1, f32[2,1,6]{2,1,0:T(1,128)} %weights.1, s32[1,6]{1,0:T(1,128)} %valid.1, f32[27,31,31]{2,1,0:T(8,128)} %basis.1, ...), custom_call_target="tpu_custom_call" | custom-call | tf_op jit(solution)/shard_map/pallas_call | solution.py:396
  25.0 1.6 %div.3 = f32[1,6,32,128]{3,2,1,0:T(8,128)} divide(f32[1,6,32,128]{3,2,1,0:T(8,128)} %get-tuple-element.7, f32[1,6,32,128]{3,2,1,0:T(8,128)} %get-tuple-element.8) | non-fusion elementwise | flops 24576 | bytes 294912 | tf_op jit(solution)/shard_map/div | solution.py:443

commit v5 on v4

--- a/solution.py
+++ b/solution.py
@@ -19,6 +19,7 @@
 KW = 31
 HALF = 15
 NB = 27
+AFTER = 19
 GROUP = 8
 DOTS = 32
 MAXOFF = 4
@@ -45,7 +46,6 @@
     coefs,
     background,
     out,
-    tally_out,
     own,
     tiles,
     edges,
@@ -134,7 +134,16 @@
 
     copies = []
 
-    def send(src, dst, peer):
+    def always(action):
+        action()
+
+    def to_above(action):
+        pl.when(r > 0)(action)
+
+    def to_below(action):
+        pl.when(r < row_count - 1)(action)
+
+    def send(src, dst, peer, out=always, back=always):
         i = len(copies)
         copy = pltpu.make_async_remote_copy(
             src_ref=src,
@@ -144,15 +153,25 @@
             device_id=peer,
             device_id_type=MESH,
         )
-        copy.start()
-        copies.append(copy)
-
-    low_rows, high_rows = pl.ds(0, ABOVE), pl.ds(ABOVE + BAND, BELOW)
-    send(own.at[:, pl.ds(0, BELOW), :], tiles.at[pl.ds(0, TILES), high_rows, :], (p, row(-1)))
+        out(lambda: copy.start())
+        copies.append((copy, out, back))
+
+    def arrived(group):
+        for copy, out_of, back in group:
+            back(lambda copy=copy: copy.wait_recv())
+
+    low_rows, high_rows = pl.ds(ABOVE - HALF, HALF), pl.ds(ABOVE + BAND, AFTER)
+    send(own.at[:, pl.ds(0, AFTER), :], tiles.at[pl.ds(0, TILES), high_rows, :],
+        (p, row(-1)),
+        to_above,
+        to_below,
+    )
     send(
-        own.at[:, pl.ds(BAND - ABOVE, ABOVE), :],
+        own.at[:, pl.ds(BAND - HALF, HALF), :],
         tiles.at[pl.ds(0, TILES), low_rows, :],
         (p, row(1)),
+        to_below,
+        to_above,
     )
     for j in range(1, SPAN):
         send(floats.at[0], floats.at[j], (det(j), r))
@@ -187,12 +206,18 @@
 
     for side, j, at in ((0, 1, LEFT), (1, -1, RIGHT)):
         send(
-            edges.at[side, pl.ds(0, BELOW), :], tiles.at[at, high_rows, :], (det(j), row(-1))
+            edges.at[side, pl.ds(0, AFTER), :],
+            tiles.at[at, high_rows, :],
+            (det(j), row(-1)),
+            to_above,
+            to_below,
         )
         send(
-            edges.at[side, pl.ds(BAND - ABOVE, ABOVE), :],
+            edges.at[side, pl.ds(BAND - HALF, HALF), :],
             tiles.at[at, low_rows, :],
             (det(j), row(1)),
+            to_below,
+            to_above,
         )
         send(edges.at[side], tiles.at[at, pl.ds(ABOVE, BAND), :], (det(j), r))
     for j in range(1, SPAN):
@@ -203,16 +228,21 @@
         )
 
 
-    def mirrored(q, coefficient):
-        total = coefficient(0) * basis_v[0]
-        for k in range(1, NB):
-            total = total + coefficient(k) * basis_v[k]
-        taps[pl.ds(0, KW), pl.ds(0, KW)] = total
-        high, low = split(taps[...])
+    def mirrored(first, last, coefficient):
+        halves = []
+        for q in range(first, last):
+            total = coefficient(q, 0) * basis_v[0]
+            for k in range(1, NB):
+                total = total + coefficient(q, k) * basis_v[k]
+            taps[q, pl.ds(0, KW), pl.ds(0, KW)] = total
+        for q in range(first, last):
+            halves += split(taps[q])
         both = jnp.dot(
-            jnp.concatenate([high, low], axis=0), mirror, preferred_element_type=jnp.float32
-        )
-        taps_back[q] = both[:BAND] + both[BAND:]
+            jnp.concatenate(halves, axis=0), mirror, preferred_element_type=jnp.float32
+        )
+        for q in range(first, last):
+            at = 2 * BAND * (q - first)
+            taps_back[q] = both[at : at + BAND] + both[at + BAND : at + 2 * BAND]
 
     def toeplitz(q, a, bands, place):
         line = jnp.broadcast_to(taps_back[q, pl.ds(a, 1), :], (8, TILE))
@@ -241,24 +271,21 @@
     rows128 = lax.broadcasted_iota(jnp.int32, (TILE, TILE), 0)
     cols128 = lax.broadcasted_iota(jnp.int32, (TILE, TILE), 1)
     mirror = jnp.where(lax.rem(rows128 + cols128, TILE) == 0, 1.0, 0.0).astype(jnp.float32)
-    taps[...] = jnp.zeros((BAND, TILE), jnp.float32)
+    taps[...] = jnp.zeros((SPAN, BAND, TILE), jnp.float32)
     load_basis.wait()
-    mirrored(0, lambda k: coefs_s[0, k])
+    mirrored(0, 1, lambda q, k: coefs_s[0, k])
     toeplitz_first_pair(0)
-    for copy in copies[2:8]:
-        copy.wait_recv()
+    arrived(copies[2:8])
     to_float = pltpu.make_async_copy(floats, float_s, local_sem.at[3])
     to_int = pltpu.make_async_copy(ints, int_s, local_sem.at[4])
     to_float.start()
     to_int.start()
     to_float.wait()
     to_int.wait()
-    for q in range(1, SPAN):
-        mirrored(q, lambda k, q=q: float_s[q, 0, k])
+    mirrored(1, SPAN, lambda q, k: float_s[q, 0, k])
     toeplitz_first_pair(1)
     load_tiles.wait()
-    for copy in copies[:2] + copies[8:14]:
-        copy.wait_recv()
+    arrived(copies[:2] + copies[8:14])
 
     eight = lax.broadcasted_iota(jnp.int32, (2 * BAND, TILE), 0)
     wide = lax.broadcasted_iota(jnp.int32, (2 * BAND, TILE), 1)
@@ -349,8 +376,7 @@
     convolve(1, bands_odd)
 
     load_seen.wait()
-    for copy in copies[14:]:
-        copy.wait_recv()
+    arrived(copies[14:])
 
     down = lax.broadcasted_iota(jnp.int32, (BAND, TILE), 0) + r * BAND
     column = lax.broadcasted_iota(jnp.int32, (BAND, TILE), 1)
@@ -378,11 +404,10 @@
         for slot, residual in parts:
             total = total + jnp.where(slot == s, residual, 0.0)
             tally = tally + jnp.where(slot == s, 1.0, 0.0)
-        out[0, s] = total
-        tally_out[0, s] = jnp.full((BAND, TILE), jnp.maximum(tally, 1.0), jnp.float32)
-
-    for copy in copies:
-        copy.wait_send()
+        out[0, s] = total / jnp.maximum(tally, 1.0)
+
+    for copy, out_of, back in copies:
+        out_of(lambda copy=copy: copy.wait_send())
 
 
 def solution(mesh):
@@ -393,14 +418,11 @@
     ):
         vmem = pl.BlockSpec(memory_space=pltpu.VMEM)
         hbm = pl.BlockSpec(memory_space=pltpu.HBM)
-        total, tally = pl.pallas_call(
+        return pl.pallas_call(
             functools.partial(kernel, det_count, row_count),
-            out_shape=(
-                jax.ShapeDtypeStruct(template.shape, jnp.float32),
-                jax.ShapeDtypeStruct(template.shape, jnp.float32),
-            ),
+            out_shape=jax.ShapeDtypeStruct(template.shape, jnp.float32),
             in_specs=[hbm] * 8 + [pl.BlockSpec(memory_space=pltpu.SMEM)],
-            out_specs=(vmem, vmem),
+            out_specs=vmem,
             scratch_shapes=[
                 pltpu.VMEM((TILES, BAND, TILE), jnp.float32),
                 pltpu.VMEM((ZERO_TILE + 1, DEEP, TILE), jnp.float32),
@@ -411,7 +433,7 @@
                 pltpu.VMEM((2, BAND, TILE, 2 * TILE), jnp.bfloat16),
                 pltpu.VMEM((NB, KW, KW), jnp.float32),
                 pltpu.VMEM((SPAN, (CAP + 1) * BAND, 2 * TILE), jnp.float32),
-                pltpu.VMEM((BAND, TILE), jnp.float32),
+                pltpu.VMEM((SPAN, BAND, TILE), jnp.float32),
                 pltpu.VMEM((SPAN, BAND, TILE), jnp.float32),
                 pltpu.VMEM((SPAN, 1, TILE), jnp.float32),
                 pltpu.VMEM((SPAN, 1, TILE), jnp.int32),
@@ -440,7 +462,6 @@
             coefs,
             background,
         )
-        return total / tally
 
     in_specs = (
         P("det", "row", None),

time: 26.8 us -> 26.7 us (level)
  other arithmetic: 1.6 us -> 0 us
  local copies, waits for them, and re-layouts: 0 us -> 1.54 us
    div x1 -> x0, other arithmetic: 1.6 us -> none  [body(): return total / tally]
    unnamed x0 -> x1, local copies, waits for them, and re-layouts: none -> 1.54 us
where the time goes in v5:
time: 26.7 us; the launch traced here: 26.5 us
  Pallas kernels  24.3 us (91%)
  local copies, waits for them, and re-layouts  1.54 us (6%)
  between operations  0.66 us (2%)
    pallas_call x1, Pallas kernels, body(): pl.pallas_call(functools.partial(kernel, det_count, row_count), out_shape...  24.3 us
    unnamed x1, local copies, waits for them, and re-layouts  1.54 us

profile of v5, /device:TPU:1, one launch (start us, length us, event | category | flops | bytes accessed | tf_op | source)
XLA Modules:
  0.0 26.5 jit_solution(6595016341649588861)
XLA Ops:
  0.7 24.3 %shard_map.91 = f32[1,6,32,128]{3,2,1,0:T(8,128)} custom-call(f32[1,32,768]{2,1,0:T(8,128)} %science.1, f32[1,6,32,128]{3,2,1,0:T(8,128)} %template.1, s32[6,128]{1,0:T(8,128)} %bitcast.1, s32[2,1,6]{2,1,0:T(1,128)} %offsets.1, f32[2,1,6]{2,1,0:T(1,128)} %weights.1, s32[1,6]{1,0:T(1,128)} %valid.1, f32[27,31,31]{2,1,0:T(8,128)} %basis.1, f32[1,27]{1,0:T(1,128)} %coefs.1, ...), custom_call_target="tpu_custom_call" | custom-call | tf_op jit(solution)/shard_map/pallas_call | solution.py:421
  25.0 1.5 %copy.12 = f32[1,6,32,128]{3,2,1,0:T(8,128)} copy(f32[1,6,32,128]{3,2,1,0:T(8,128)} %shard_map.91) | data formatting | bytes 196608

commit v6 on v5

--- a/solution.py
+++ b/solution.py
@@ -105,9 +105,9 @@
         )
     ):
         small.append(pltpu.make_async_copy(src, dst, local_sem.at[6 + i]))
-    load_own.start()
     for copy in small:
         copy.start()
+    load_own.start()
     load_basis.start()
     load_tiles.start()
     load_seen.start()
@@ -129,7 +129,6 @@
     floats[0] = packed
     ints[0] = whole
 
-    load_own.wait()
     pl.semaphore_wait(barrier, len(peers))
 
     copies = []
@@ -160,6 +159,10 @@
         for copy, out_of, back in group:
             back(lambda copy=copy: copy.wait_recv())
 
+    for j in range(1, SPAN):
+        send(floats.at[0], floats.at[j], (det(j), r))
+        send(ints.at[0], ints.at[j], (det(j), r))
+    load_own.wait()
     low_rows, high_rows = pl.ds(ABOVE - HALF, HALF), pl.ds(ABOVE + BAND, AFTER)
     send(own.at[:, pl.ds(0, AFTER), :], tiles.at[pl.ds(0, TILES), high_rows, :],
         (p, row(-1)),
@@ -173,9 +176,6 @@
         to_below,
         to_above,
     )
-    for j in range(1, SPAN):
-        send(floats.at[0], floats.at[j], (det(j), r))
-        send(ints.at[0], ints.at[j], (det(j), r))
 
     runs = []
     for q in range(SPAN):
@@ -275,7 +275,7 @@
     load_basis.wait()
     mirrored(0, 1, lambda q, k: coefs_s[0, k])
     toeplitz_first_pair(0)
-    arrived(copies[2:8])
+    arrived(copies[:6])
     to_float = pltpu.make_async_copy(floats, float_s, local_sem.at[3])
     to_int = pltpu.make_async_copy(ints, int_s, local_sem.at[4])
     to_float.start()
@@ -285,7 +285,7 @@
     mirrored(1, SPAN, lambda q, k: float_s[q, 0, k])
     toeplitz_first_pair(1)
     load_tiles.wait()
-    arrived(copies[:2] + copies[8:14])
+    arrived(copies[6:14])
 
     eight = lax.broadcasted_iota(jnp.int32, (2 * BAND, TILE), 0)
     wide = lax.broadcasted_iota(jnp.int32, (2 * BAND, TILE), 1)

time: 26.7 us -> 26.7 us (level)
  no operation moved by 1% of the time
where the time goes in v6:
time: 26.7 us; the launch traced here: 26.5 us
  Pallas kernels  24.3 us (91%)
  local copies, waits for them, and re-layouts  1.54 us (6%)
  between operations  0.66 us (2%)
    pallas_call x1, Pallas kernels, body(): pl.pallas_call(functools.partial(kernel, det_count, row_count), out_shape...  24.3 us
    unnamed x1, local copies, waits for them, and re-layouts  1.54 us

profile of v6, /device:TPU:1, one launch (start us, length us, event | category | flops | bytes accessed | tf_op | source)
XLA Modules:
  0.0 26.5 jit_solution(3723208838841466288)
XLA Ops:
  0.7 24.3 %shard_map.91 = f32[1,6,32,128]{3,2,1,0:T(8,128)} custom-call(f32[1,32,768]{2,1,0:T(8,128)} %science.1, f32[1,6,32,128]{3,2,1,0:T(8,128)} %template.1, s32[6,128]{1,0:T(8,128)} %bitcast.1, s32[2,1,6]{2,1,0:T(1,128)} %offsets.1, f32[2,1,6]{2,1,0:T(1,128)} %weights.1, s32[1,6]{1,0:T(1,128)} %valid.1, f32[27,31,31]{2,1,0:T(8,128)} %basis.1, f32[1,27]{1,0:T(1,128)} %coefs.1, ...), custom_call_target="tpu_custom_call" | custom-call | tf_op jit(solution)/shard_map/pallas_call | solution.py:421
  25.0 1.5 %copy.12 = f32[1,6,32,128]{3,2,1,0:T(8,128)} copy(f32[1,6,32,128]{3,2,1,0:T(8,128)} %shard_map.91) | data formatting | bytes 196608

commit v7 on v6

--- a/solution.py
+++ b/solution.py
@@ -275,6 +275,75 @@
     load_basis.wait()
     mirrored(0, 1, lambda q, k: coefs_s[0, k])
     toeplitz_first_pair(0)
+    load_tiles.wait()
+    arrived(copies[6:14])
+    eight = lax.broadcasted_iota(jnp.int32, (2 * BAND, TILE), 0)
+    wide = lax.broadcasted_iota(jnp.int32, (2 * BAND, TILE), 1)
+    line_at = eight + (r * BAND - HALF)
+    tail = wide < HALF
+    def own_shift(c):
+        return (
+            (offsets_s[0, 0, c], offsets_s[1, 0, c]),
+            (weights_s[0, 0, c], weights_s[1, 0, c]),
+        )
+
+    def sent_shift(q, c):
+        return (
+            (int_s[q, 0, c], int_s[q, 0, 6 + c]),
+            (float_s[q, 0, 28 + c], float_s[q, 0, 34 + c]),
+        )
+
+    def warp(kernels):
+        for q in kernels:
+            start, length, first = runs[q]
+            before = former = None
+            for m in range(CAP + 2):
+                c = jnp.clip(start + (m - 1), 0, TILES - 1)
+                shifts, mixes = own_shift(c) if q == 0 else sent_shift(q, c)
+                row_shift = jnp.clip(shifts[0], 0, MAXOFF - 1)
+                col_shift = shifts[1]
+                row_weight, col_weight = mixes
+                turn = jnp.int32(HALF + TILE) - col_shift
+                last_lane = TILE - 1
+                if m == 0:
+                    index = LEFT if q > 0 else ZERO_TILE
+                    last_lane = STRIP * q - 1 if q > 0 else TILE - 1
+                    turn = turn - STRIP * q
+                else:
+                    edge = RIGHT if q < SPAN - 1 else ZERO_TILE
+                    index = jnp.where(
+                        m <= length, first + (m - 1), jnp.where(m == length + 1, edge, ZERO_TILE)
+                    )
+                    index = jnp.clip(index, 0, ZERO_TILE)
+                    if q > 0:
+                        turn = turn - jnp.where(m > length, STRIP * q, 0)
+                upper = tiles[index, pl.ds(1 + row_shift, 2 * BAND), :]
+                lower = tiles[index, pl.ds(2 + row_shift, 2 * BAND), :]
+                limit = row_count * BAND - row_shift
+                upper = jnp.where(line_at < limit, (1.0 - row_weight) * upper, 0.0)
+                lower = jnp.where(line_at < limit - 1, row_weight * lower, 0.0)
+                mixed = jnp.where(line_at >= 0, upper + lower, 0.0)
+                last = jnp.broadcast_to(mixed[:, last_lane : last_lane + 1], (2 * BAND, TILE))
+                left = pltpu.roll(mixed, lax.rem(turn, TILE), 1)
+                left = jnp.where(tail & (wide > HALF - 1 - col_shift), last, left)
+                following = pltpu.roll(mixed, lax.rem(turn - 1, TILE), 1)
+                following = jnp.where(tail & (wide > HALF - 2 - col_shift), last, following)
+                now = (1.0 - col_weight) * left + col_weight * following
+                if m > 0:
+                    t = m - 1
+                    here = jnp.where(tail, before, now)
+                    window = here
+                    if t > 0:
+                        skip = TILE - STEP
+                        window = jnp.where(wide >= TILE - skip * t, former, here)
+                        window = pltpu.roll(window, skip * t, 1)
+                    high, low = split(window)
+                    images[q, 0, t] = high
+                    images[q, 1, t] = low
+                    former = here
+                before = now
+
+    warp(range(1))
     arrived(copies[:6])
     to_float = pltpu.make_async_copy(floats, float_s, local_sem.at[3])
     to_int = pltpu.make_async_copy(ints, int_s, local_sem.at[4])
@@ -284,60 +353,8 @@
     to_int.wait()
     mirrored(1, SPAN, lambda q, k: float_s[q, 0, k])
     toeplitz_first_pair(1)
-    load_tiles.wait()
-    arrived(copies[6:14])
-
-    eight = lax.broadcasted_iota(jnp.int32, (2 * BAND, TILE), 0)
-    wide = lax.broadcasted_iota(jnp.int32, (2 * BAND, TILE), 1)
-    line_at = eight + (r * BAND - HALF)
-    tail = wide < HALF
-    for q in range(SPAN):
-        start, length, first = runs[q]
-        before = former = None
-        for m in range(CAP + 2):
-            c = jnp.clip(start + (m - 1), 0, TILES - 1)
-            row_shift = jnp.clip(int_s[q, 0, c], 0, MAXOFF - 1)
-            col_shift = int_s[q, 0, 6 + c]
-            row_weight, col_weight = float_s[q, 0, 28 + c], float_s[q, 0, 34 + c]
-            turn = jnp.int32(HALF + TILE) - col_shift
-            last_lane = TILE - 1
-            if m == 0:
-                index = LEFT if q > 0 else ZERO_TILE
-                last_lane = STRIP * q - 1 if q > 0 else TILE - 1
-                turn = turn - STRIP * q
-            else:
-                edge = RIGHT if q < SPAN - 1 else ZERO_TILE
-                index = jnp.where(
-                    m <= length, first + (m - 1), jnp.where(m == length + 1, edge, ZERO_TILE)
-                )
-                index = jnp.clip(index, 0, ZERO_TILE)
-                if q > 0:
-                    turn = turn - jnp.where(m > length, STRIP * q, 0)
-            upper = tiles[index, pl.ds(1 + row_shift, 2 * BAND), :]
-            lower = tiles[index, pl.ds(2 + row_shift, 2 * BAND), :]
-            limit = row_count * BAND - row_shift
-            upper = jnp.where(line_at < limit, (1.0 - row_weight) * upper, 0.0)
-            lower = jnp.where(line_at < limit - 1, row_weight * lower, 0.0)
-            mixed = jnp.where(line_at >= 0, upper + lower, 0.0)
-            last = jnp.broadcast_to(mixed[:, last_lane : last_lane + 1], (2 * BAND, TILE))
-            left = pltpu.roll(mixed, lax.rem(turn, TILE), 1)
-            left = jnp.where(tail & (wide > HALF - 1 - col_shift), last, left)
-            following = pltpu.roll(mixed, lax.rem(turn - 1, TILE), 1)
-            following = jnp.where(tail & (wide > HALF - 2 - col_shift), last, following)
-            now = (1.0 - col_weight) * left + col_weight * following
-            if m > 0:
-                t = m - 1
-                here = jnp.where(tail, before, now)
-                window = here
-                if t > 0:
-                    skip = TILE - STEP
-                    window = jnp.where(wide >= TILE - skip * t, former, here)
-                    window = pltpu.roll(window, skip * t, 1)
-                high, low = split(window)
-                images[q, 0, t] = high
-                images[q, 1, t] = low
-                former = here
-            before = now
+
+    warp(range(1, SPAN))
 
     rest = jnp.zeros((TILE, TILE), jnp.bfloat16)
     model_v[...] = jnp.zeros_like(model_v)

time: 26.7 us -> 26.9 us (level)
  no operation moved by 1% of the time
where the time goes in v7:
time: 26.9 us; the launch traced here: 26.7 us
  Pallas kernels  24.5 us (91%)
  local copies, waits for them, and re-layouts  1.54 us (6%)
  between operations  0.66 us (2%)
    pallas_call x1, Pallas kernels, body(): pl.pallas_call(functools.partial(kernel, det_count, row_count), out_shape...  24.5 us
    unnamed x1, local copies, waits for them, and re-layouts  1.54 us

profile of v7, /device:TPU:1, one launch (start us, length us, event | category | flops | bytes accessed | tf_op | source)
XLA Modules:
  0.0 26.7 jit_solution(13263007565581897836)
XLA Ops:
  0.7 24.5 %shard_map.91 = f32[1,6,32,128]{3,2,1,0:T(8,128)} custom-call(f32[1,32,768]{2,1,0:T(8,128)} %science.1, f32[1,6,32,128]{3,2,1,0:T(8,128)} %template.1, s32[6,128]{1,0:T(8,128)} %bitcast.1, s32[2,1,6]{2,1,0:T(1,128)} %offsets.1, f32[2,1,6]{2,1,0:T(1,128)} %weights.1, s32[1,6]{1,0:T(1,128)} %valid.1, f32[27,31,31]{2,1,0:T(8,128)} %basis.1, f32[1,27]{1,0:T(1,128)} %coefs.1, ...), custom_call_target="tpu_custom_call" | custom-call | tf_op jit(solution)/shard_map/pallas_call | solution.py:438
  25.2 1.5 %copy.12 = f32[1,6,32,128]{3,2,1,0:T(8,128)} copy(f32[1,6,32,128]{3,2,1,0:T(8,128)} %shard_map.91) | data formatting | bytes 196608
